TPU v7x, 32 devices: a 4x4x1 block of a 4x4x8 slice. The times are simulated.
32 devices in a mesh: rep: 1 (over z), dp: 32 (over x, y, core).
Axes of the slice: x: 4, y: 4, z: 1, core: 2. Of those that a mesh axis runs over, the one named last changes fastest.
The devices are a block of a 4x4x8 slice.
Arguments:
- x: bfloat16 [32, 1024, 512], P(('rep', 'dp'))
- dy: bfloat16 [32, 1024, 512], P(('rep', 'dp'))
- w_gate: bfloat16 [2, 512, 8192], replicated
- w_up: bfloat16 [2, 512, 8192], replicated
- w_down: bfloat16 [2, 8192, 512], replicated
- m_w_gate: float32 [2, 512, 8192], P(None, 'dp')
- m_w_up: float32 [2, 512, 8192], P(None, 'dp')
- m_w_down: float32 [2, 8192, 512], P(None, 'dp')
- v_w_gate: float32 [2, 512, 8192], P(None, 'dp')
- v_w_up: float32 [2, 512, 8192], P(None, 'dp')
- v_w_down: float32 [2, 8192, 512], P(None, 'dp')
Outputs:
- output 1: bfloat16 [2, 512, 8192], P('rep')
- output 2: bfloat16 [2, 512, 8192], P('rep')
- output 3: bfloat16 [2, 8192, 512], P('rep')
- output 4: float32 [2, 512, 8192], P('rep', 'dp')
- output 5: float32 [2, 512, 8192], P('rep', 'dp')
- output 6: float32 [2, 8192, 512], P('rep', 'dp')
- output 7: float32 [2, 512, 8192], P('rep', 'dp')
- output 8: float32 [2, 512, 8192], P('rep', 'dp')
- output 9: float32 [2, 8192, 512], P('rep', 'dp')
All inputs are finite; a program needn't handle non-finite values.
Results may differ from a plain program's by a relative error of at most 0.022.
Values are sent between devices in bfloat16 or wider.
A program may use at most 768 MiB of HBM per device.

v0:
```python
import jax
import jax.numpy as jnp
from jax import lax

NAMES = ("w_gate", "w_up", "w_down")


def matmul(a, w):
    return jnp.dot(a, w, preferred_element_type=jnp.float32).astype(jnp.bfloat16)


def normed(h):
    wide = h.astype(jnp.float32)
    scale = lax.rsqrt(jnp.mean(wide**2, -1, keepdims=True) + 1e-6)
    return (wide * scale).astype(jnp.bfloat16)


def layer(h, w):
    a = normed(h)
    gate = jnp.dot(a, w["w_gate"], preferred_element_type=jnp.float32)
    up = jnp.dot(a, w["w_up"], preferred_element_type=jnp.float32)
    return h + matmul((jax.nn.silu(gate) * up).astype(jnp.bfloat16), w["w_down"])


def adamw(w, m, v, g):
    m = 0.9 * m + 0.1 * g
    v = 0.95 * v + 0.05 * g * g
    step = m * lax.rsqrt(v + 1e-8) + 0.1 * w
    return (w - 0.02 * step).astype(jnp.bfloat16), m, v


def clipped(gradients, sum_of_squares, count):
    factor = jnp.minimum(1.0, 0.5 * lax.rsqrt(sum_of_squares / count + 1e-30))
    return [g * factor for g in gradients]


def stack(weights, h):
    for number in range(weights["w_gate"].shape[0]):
        h = layer(h, {name: w[number] for name, w in weights.items()})
    return h


def solution(mesh):
    groups = mesh.shape["rep"]

    def step(x, dy, *arrays):
        weights, m, v = (arrays[i : i + 3] for i in (0, 3, 6))
        x, dy = (t.reshape(groups, -1, *t.shape[1:]) for t in (x, dy))

        def of_a_group(x, dy):
            _, back = jax.vjp(lambda w: stack(w, x), dict(zip(NAMES, weights, strict=True)))
            by_weights = back(dy)[0]
            gradients = [by_weights[name].astype(jnp.float32) for name in NAMES]
            gradients = clipped(gradients, sum(jnp.sum(g * g) for g in gradients), sum(g.size for g in gradients))
            new = [adamw(w.astype(jnp.float32), m, v, g) for w, m, v, g in zip(weights, m, v, gradients, strict=True)]
            return tuple(one[which] for which in range(3) for one in new)

        return tuple(t.reshape(-1, *t.shape[2:]) for t in jax.vmap(of_a_group)(x, dy))

    return step
```

profile of v0, /device:TPU:97, one launch (start us, length us, event | category | flops | bytes accessed | tf_op | source)
XLA Modules:
  0.0 1199.8 jit_solution(1594746858259066677)
XLA Ops:
  7.2 0.1 reduce-scatter.29.cloned.1.call-start
  7.3 1.5 fusion.59
  8.8 1.5 copy
  10.3 19.0 %fusion.47 = f32[1024,8192]{1,0:T(8,128)} fusion(bf16[2,512,8192]{2,1,0:T(8,128)(2,1)} %param, bf16[1,1024,512]{2,1,0:T(8,128)(2,1)} %param.4, f32[1024]{0:T(1024)S(1)} %add_rsqrt_fusion), kind=kOutput, calls=%fused_computation.57 | convolution fusion | flops 8591507456 | bytes 42995712 | tf_op jit(solution)/vmap(jvp())/dot_general | solution.py:20
  29.3 18.0 %fusion.45 = f32[1024,8192]{1,0:T(8,128)} fusion(bf16[2,512,8192]{2,1,0:T(8,128)(2,1)} %param.5, bf16[1,1024,512]{2,1,0:T(8,128)(2,1)S(1)} %copy-done.3, f32[1024]{0:T(1024)S(1)} %add_rsqrt_fusion), kind=kOutput, calls=%fused_computation.55 | convolution fusion | flops 8591507456 | bytes 42995712 | tf_op jit(solution)/vmap(jvp())/dot_general | solution.py:21
  47.3 27.4 %fusion.26 = bf16[1024,8192]{1,0:T(8,128)(2,1)} fusion(f32[1024,8192]{1,0:T(8,128)} %fusion.45, f32[1024,8192]{1,0:T(8,128)} %fusion.47), kind=kLoop, calls=%fused_computation.35 | loop fusion | flops 50331648 | bytes 83886080
  74.7 14.9 %fusion.63 = (f32[1024]{0:T(1024)S(1)}, bf16[1,1024,512]{1,2,0:T(8,128)(2,1)S(1)}) fusion(bf16[1,1024,512]{1,2,0:T(8,128)(2,1)S(1)} %copy, bf16[1024,8192]{1,0:T(8,128)(2,1)} %fusion.26, bf16[2,8192,512]{2,1,0:T(8,128)(2,1)} %param.3), kind=kOutput, calls=%fused_computation.80 | convolution fusion | flops 8592555008 | bytes 27267072 | tf_op jit(solution)/vmap(jvp())/dot_general | solution.py:9
  89.7 19.1 %fusion.35 = f32[1024,8192]{1,0:T(8,128)} fusion(bf16[2,512,8192]{2,1,0:T(8,128)(2,1)} %param, bf16[1,1024,512]{1,2,0:T(8,128)(2,1)S(1)} %get-tuple-element.10, f32[1024]{0:T(1024)S(1)} %bitcast.344), kind=kOutput, calls=%fused_computation.45 | convolution fusion | flops 8591507456 | bytes 42995712 | tf_op jit(solution)/vmap(jvp())/dot_general | solution.py:20
  108.8 18.8 %fusion.39 = f32[1024,8192]{1,0:T(8,128)} fusion(bf16[2,512,8192]{2,1,0:T(8,128)(2,1)} %param.5, bf16[1,1024,512]{1,2,0:T(8,128)(2,1)S(1)} %get-tuple-element.10, f32[1024]{0:T(1024)S(1)} %bitcast.345), kind=kOutput, calls=%fused_computation.49 | convolution fusion | flops 8591507456 | bytes 42995712 | tf_op jit(solution)/vmap(jvp())/dot_general | solution.py:21
  127.6 15.2 %convolution_convert_fusion.1 = bf16[1024,8192]{1,0:T(8,128)(2,1)} fusion(bf16[2,8192,512]{2,1,0:T(8,128)(2,1)} %param.3, bf16[1,1024,512]{2,1,0:T(8,128)(2,1)S(1)} %copy-done.7), kind=kOutput, calls=%fused_computation.44 | convolution fusion | flops 8598323200 | bytes 26214400 | tf_op jit(solution)/vmap(transpose(jvp()))/dot_general | solution.py:9
  142.9 0.5 copy.1
  143.4 33.4 %fusion.6 = bf16[1024,8192]{1,0:T(8,128)(2,1)} fusion(f32[1024,8192]{1,0:T(8,128)} %fusion.35, f32[1024,8192]{1,0:T(8,128)} %fusion.39, bf16[1024,8192]{1,0:T(8,128)(2,1)} %convolution_convert_fusion.1), kind=kLoop, calls=%fused_computation.11 | loop fusion | flops 100663296 | bytes 100663296
  176.8 15.6 %fusion.69 = bf16[1024,512]{0,1:T(8,128)(2,1)} fusion(bf16[1024,8192]{1,0:T(8,128)(2,1)} %fusion.6, bf16[2,512,8192]{2,1,0:T(8,128)(2,1)} %param), kind=kOutput, calls=%fused_computation.87 | convolution fusion | flops 8589934592 | bytes 26214400 | tf_op jit(solution)/vmap(transpose(jvp()))/dot_general | solution.py:20
  192.4 24.3 %fusion.65 = (f32[1024]{0:T(1024)S(1)}, bf16[1,1024,512]{1,2,0:T(8,128)(2,1)}) fusion(bf16[1,1024,512]{1,2,0:T(8,128)(2,1)S(1)} %get-tuple-element.10, bf16[1024,512]{0,1:T(8,128)(2,1)} %fusion.69, bf16[2,512,8192]{2,1,0:T(8,128)(2,1)} %param.5, bf16[1024,8192]{1,0:T(8,128)(2,1)} %convolution_convert_fusion.1, f32[1024,8192]{1,0:T(8,128)} %fusion.35), kind=kOutput, calls=%fused_computation.82 | convolution fusion | flops 8643410944 | bytes 61870080 | tf_op jit(solution)/vmap(transpose(jvp()))/dot_general | solution.py:21
  216.7 2.9 fusion.122
  219.6 16.2 %fusion.146 = f32[512,8192]{0,1:T(8,128)} fusion(bf16[1024,512]{0,1:T(8,128)(2,1)} %fusion.122, bf16[1024,8192]{1,0:T(8,128)(2,1)} %fusion.26), kind=kOutput, calls=%fused_computation.162 | convolution fusion | flops 8589934592 | bytes 34603008 | tf_op jit(solution)/vmap(transpose(jvp()))/dot_general | solution.py:9
  235.8 0.1 reduce-scatter.29.cloned.1.call-update
  235.8 0.1 reduce-scatter.27.cloned.1.call-start
  235.9 29.4 %fusion.28 = f32[8192,512]{1,0:T(8,128)} fusion(f32[1024,8192]{1,0:T(8,128)} %fusion.39, f32[1024,8192]{1,0:T(8,128)} %fusion.35, bf16[1,1024,512]{2,1,0:T(8,128)(2,1)S(1)} %copy-done.7), kind=kOutput, calls=%fused_computation.37 | convolution fusion | flops 8640266240 | bytes 84934656 | tf_op jit(solution)/vmap(transpose(jvp()))/dot_general | solution.py:9
  265.3 0.1 reduce-scatter.27.cloned.1.call-update
  265.4 0.1 reduce-scatter.25.cloned.1.call-start
  265.5 1.1 copy-done.9
  266.6 16.2 %convolution_convert_fusion = bf16[1024,8192]{1,0:T(8,128)(2,1)} fusion(bf16[1024,512]{0,1:T(8,128)(2,1)S(1)} %copy-done.9, bf16[2,8192,512]{2,1,0:T(8,128)(2,1)} %param.3), kind=kOutput, calls=%fused_computation.43 | convolution fusion | flops 8598323200 | bytes 26214400 | tf_op jit(solution)/vmap(transpose(jvp()))/dot_general | solution.py:9
  282.8 26.6 %fusion.2 = f32[8192,512]{0,1:T(8,128)} fusion(bf16[1024,8192]{1,0:T(8,128)(2,1)} %convolution_convert_fusion, f32[1024,8192]{1,0:T(8,128)} %fusion.47, bf16[1,1024,512]{2,1,0:T(8,128)(2,1)S(1)} %copy-done.4, f32[1024]{0:T(1024)S(1)} %copy-done.11), kind=kOutput, calls=%fused_computation.8 | convolution fusion | flops 8641839104 | bytes 68161536 | tf_op jit(solution)/vmap(transpose(jvp()))/dot_general | solution.py:21
  309.4 0.1 reduce-scatter.25.cloned.1.call-update
  309.5 0.1 reduce-scatter.23.cloned.1.call-start
  309.6 1.1 copy-done.2
  310.6 26.6 %fusion.22 = f32[8192,512]{0,1:T(8,128)} fusion(bf16[1024,8192]{1,0:T(8,128)(2,1)} %convolution_convert_fusion.1, f32[1024,8192]{1,0:T(8,128)} %fusion.35, bf16[1,1024,512]{1,2,0:T(8,128)(2,1)S(1)} %copy-done.2, f32[1024]{0:T(1024)S(1)} %bitcast.347), kind=kOutput, calls=%fused_computation.33 | convolution fusion | flops 8641839104 | bytes 68161536 | tf_op jit(solution)/vmap(transpose(jvp()))/dot_general | solution.py:21
  337.2 0.1 reduce-scatter.23.cloned.1.call-update
  337.3 0.1 reduce-scatter.21.cloned.1.call-start
  337.4 35.5 %fusion.10 = f32[8192,512]{0,1:T(8,128)} fusion(f32[1024,8192]{1,0:T(8,128)} %fusion.47, f32[1024,8192]{1,0:T(8,128)} %fusion.45, bf16[1024,8192]{1,0:T(8,128)(2,1)} %convolution_convert_fusion, bf16[1,1024,512]{2,1,0:T(8,128)(2,1)S(1)} %copy-done.4, f32[1024]{0:T(1024)S(1)} %copy-done.11), kind=kOutput, calls=%fused_computation.15 | convolution fusion | flops 8683782144 | bytes 101715968 | tf_op jit(solution)/vmap(transpose(jvp()))/dot_general | solution.py:20
  372.9 0.1 reduce-scatter.21.cloned.1.call-update
  373.0 0.1 reduce-scatter.19.cloned.1.call-start
  373.1 16.2 %fusion.127 = f32[8192,512]{0,1:T(8,128)} fusion(bf16[1024,8192]{1,0:T(8,128)(2,1)} %fusion.6, bf16[1,1024,512]{1,2,0:T(8,128)(2,1)S(1)} %copy-done.2, f32[1024]{0:T(1024)S(1)} %bitcast.348), kind=kOutput, calls=%fused_computation.138 | convolution fusion | flops 8591507456 | bytes 34607104 | tf_op jit(solution)/vmap(transpose(jvp()))/dot_general | solution.py:20
  389.3 0.1 reduce-scatter.19.cloned.1.call-update
  389.3 0.1 all-gather.14.cloned.1.call-start
  389.4 1.2 convert_bitcast_fusion.3
  390.6 65.7 %reduce-scatter.27.cloned.1.call-done = f32[256,512]{1,0:T(8,128)} async-done(((f32[8192,512]{1,0:T(8,128)}), f32[256,512]{1,0:T(8,128)}) %reduce-scatter.27.cloned.1.call-update) | async-done | bytes 524304
  456.3 1.1 convert_bitcast_fusion.4
  457.4 0.9 fusion.106
  458.3 108.7 %reduce-scatter.25.cloned.1.call-done = f32[8192,16]{0,1:T(8,128)} async-done(((f32[8192,512]{0,1:T(8,128)}), f32[8192,16]{0,1:T(8,128)}) %reduce-scatter.25.cloned.1.call-update) | async-done | bytes 524304
  567.0 1.1 convert_bitcast_fusion.5
  568.0 109.4 %reduce-scatter.23.cloned.1.call-done = f32[8192,16]{0,1:T(8,128)} async-done(((f32[8192,512]{0,1:T(8,128)}), f32[8192,16]{0,1:T(8,128)}) %reduce-scatter.23.cloned.1.call-update) | async-done | bytes 524304
  677.4 1.1 convert_bitcast_fusion.6
  678.5 0.9 fusion.105
  679.4 109.1 %reduce-scatter.21.cloned.1.call-done = f32[8192,16]{0,1:T(8,128)} async-done(((f32[8192,512]{0,1:T(8,128)}), f32[8192,16]{0,1:T(8,128)}) %reduce-scatter.21.cloned.1.call-update) | async-done | bytes 524304
  788.5 1.1 convert_bitcast_fusion.7
  789.5 110.0 %reduce-scatter.19.cloned.1.call-done = f32[8192,16]{0,1:T(8,128)} async-done(((f32[8192,512]{0,1:T(8,128)}), f32[8192,16]{0,1:T(8,128)}) %reduce-scatter.19.cloned.1.call-update) | async-done | bytes 524304
  899.5 1.1 convert_bitcast_fusion.8
  900.6 0.9 fusion.104
  903.4 46.3 %all-reduce.16 = f32[]{:T(128)} all-reduce(f32[]{:T(128)S(6)} %add.114), channel_id=5, replica_groups=mesh['rep'=1,'dp'=32] {'dp'}, use_global_device_ids=true, to_apply=%region_3.4.clone | all-reduce | flops 1 | bytes 8 | tf_op jit(solution)/vmap()/reduce_sum | solution.py:54
  950.4 3.5 fusion.136
  953.9 0.1 all-gather.12.cloned.1.call-start
  954.0 3.8 fusion.134
  957.8 0.1 all-gather.10.cloned.1.call-start
  957.9 3.8 fusion.135
  961.7 58.0 %all-gather.14.cloned.1.call-done = bf16[1,2,8192,512]{3,2,1,0:T(8,128)(2,1)} async-done(((bf16[1,2,256,512]{3,2,1,0:T(8,128)(2,1)}), bf16[1,2,8192,512]{3,2,1,0:T(8,128)(2,1)}) %all-gather.14.cloned.1.call-update) | async-done | bytes 16777232 | tf_op jit(solution)/reshape | solution.py:58
  1019.7 69.4 %all-gather.12.cloned.1.call-done = bf16[1,2,512,8192]{3,2,1,0:T(8,128)(2,1)} async-done(((bf16[1,2,16,8192]{3,2,1,0:T(8,128)(2,1)}), bf16[1,2,512,8192]{3,2,1,0:T(8,128)(2,1)}) %all-gather.12.cloned.1.call-update) | async-done | bytes 16777232 | tf_op jit(solution)/reshape | solution.py:58
  1089.2 69.5 %all-gather.10.cloned.1.call-done = bf16[1,2,512,8192]{3,2,1,0:T(8,128)(2,1)} async-done(((bf16[1,2,16,8192]{3,2,1,0:T(8,128)(2,1)}), bf16[1,2,512,8192]{3,2,1,0:T(8,128)(2,1)}) %all-gather.10.cloned.1.call-update) | async-done | bytes 16777232 | tf_op jit(solution)/reshape | solution.py:58
  1158.6 16.7 %copy.7 = bf16[2,512,8192]{2,1,0:T(8,128)(2,1)} copy(bf16[2,512,8192]{2,1,0:T(8,128)(2,1)} %bitcast.343) | data formatting | bytes 33554432
  1175.3 8.5 copy.8
  1183.8 1.5 slice-done.2
  1185.4 1.2 slice-done.3
  1186.5 6.2 copy.9
  (37 shorter events, 0.3 us)
Async XLA Ops:
  7.2 382.2 %reduce-scatter.29.cloned.1.call-start = ((), (), s32[]{:S(2)}) async-start(), calls=%async_computation.14 | async-start | bytes 17301504
  10.3 19.1 %copy-start.10 = (f32[1024]{0:T(1024)}, f32[1024]{0:T(1024)S(1)}, u32[]{:S(2)}) copy-start(f32[1024]{0:T(1024)S(1)} %add_rsqrt_fusion) | copy-start | bytes 12292
  10.3 19.1 %copy-start.3 = (bf16[1,1024,512]{2,1,0:T(8,128)(2,1)S(1)}, bf16[1,1024,512]{2,1,0:T(8,128)(2,1)}, u32[]{:S(2)}) copy-start(bf16[1,1024,512]{2,1,0:T(8,128)(2,1)} %param.4) | copy-start | bytes 3145732
  89.7 127.1 %copy-start.1 = (bf16[1,1024,512]{1,2,0:T(8,128)(2,1)}, bf16[1,1024,512]{1,2,0:T(8,128)(2,1)S(1)}, u32[]{:S(2)}) copy-start(bf16[1,1024,512]{1,2,0:T(8,128)(2,1)S(1)} %get-tuple-element.10) | copy-start | bytes 3145732
  89.7 127.0 %copy-start.5 = (f32[1,1024]{1,0:T(1,128)}, f32[1,1024]{1,0:T(1,128)S(1)}, u32[]{:S(2)}) copy-start(f32[1,1024]{1,0:T(1,128)S(1)} %rsqrt.32) | copy-start | bytes 12292
  108.8 18.8 %copy-start.7 = (bf16[1,1024,512]{2,1,0:T(8,128)(2,1)S(1)}, bf16[1,1024,512]{2,1,0:T(8,128)(2,1)}, u32[]{:S(2)}) copy-start(bf16[1,1024,512]{2,1,0:T(8,128)(2,1)} %param.2) | copy-start | bytes 3145732
  235.8 220.5 %reduce-scatter.27.cloned.1.call-start = ((), (), s32[]{:S(2)}) async-start(), calls=%async_computation.13 | async-start | bytes 17301504
  265.3 1.2 copy-start.9
  265.4 17.4 %copy-start.4 = (bf16[1,1024,512]{2,1,0:T(8,128)(2,1)S(1)}, bf16[1,1024,512]{2,1,0:T(8,128)(2,1)}, u32[]{:S(2)}) copy-start(bf16[1,1024,512]{2,1,0:T(8,128)(2,1)} %param.4) | copy-start | bytes 3145732
  265.4 17.4 %copy-start.11 = (f32[1024]{0:T(1024)S(1)}, f32[1024]{0:T(1024)}, u32[]{:S(2)}) copy-start(f32[1024]{0:T(1024)} %copy-done.10) | copy-start | bytes 12292
  265.4 301.5 %reduce-scatter.25.cloned.1.call-start = ((), (), s32[]{:S(2)}) async-start(), calls=%async_computation.12 | async-start | bytes 17301504
  309.4 1.2 copy-start.2
  309.4 1.2 copy-start.6
  309.5 368.0 %reduce-scatter.23.cloned.1.call-start = ((), (), s32[]{:S(2)}) async-start(), calls=%async_computation.11 | async-start | bytes 17301504
  337.3 451.2 %reduce-scatter.21.cloned.1.call-start = ((), (), s32[]{:S(2)}) async-start(), calls=%async_computation.10 | async-start | bytes 17301504
  373.0 526.5 %reduce-scatter.19.cloned.1.call-start = ((), (), s32[]{:S(2)}) async-start(), calls=%async_computation.9 | async-start | bytes 17301504
  389.3 561.1 %copy-start.8 = (f32[2,256,512]{2,1,0:T(8,128)S(1)}, f32[2,256,512]{2,1,0:T(8,128)}, u32[]{:S(2)}) copy-start(f32[2,256,512]{2,1,0:T(8,128)} %param.10) | copy-start | bytes 3145732
  389.3 630.4 %all-gather.14.cloned.1.call-start = ((), (), s32[]{:S(2)}) async-start(), calls=%async_computation.8 | async-start | bytes 17301504 | tf_op jit(solution)/reshape | solution.py:58
  953.9 135.3 %all-gather.12.cloned.1.call-start = ((), (), s32[]{:S(2)}) async-start(), calls=%async_computation.7 | async-start | bytes 17301504 | tf_op jit(solution)/reshape | solution.py:58
  957.8 200.8 %all-gather.10.cloned.1.call-start = ((), (), s32[]{:S(2)}) async-start(), calls=%async_computation.6 | async-start | bytes 17301504 | tf_op jit(solution)/reshape | solution.py:58
  1158.6 16.7 %copy-start = (bf16[1,2,512,8192]{3,2,1,0:T(8,128)(2,1)S(1)}, bf16[1,2,512,8192]{3,2,1,0:T(8,128)(2,1)}, u32[]{:S(2)}) copy-start(bf16[1,2,512,8192]{3,2,1,0:T(8,128)(2,1)} %all-gather.12.cloned.1.call-done) | copy-start | bytes 50331652
  1158.6 25.2 %slice-start = ((s8[16777216]{0:T(1024)(128)(4,1)}), s8[4194304]{0:T(1024)(128)(4,1)S(1)}, s32[]{:S(2)}) async-start(s8[16777216]{0:T(1024)(128)(4,1)} %bitcast.339), calls=%async_computation.15 | async-start | bytes 8388608
  1158.6 25.2 %slice-start.1 = ((s8[16777216]{0:T(1024)(128)(4,1)}), s8[4194304]{0:T(1024)(128)(4,1)S(1)}, s32[]{:S(2)}) async-start(s8[16777216]{0:T(1024)(128)(4,1)} %bitcast.339), calls=%async_computation.16 | async-start | bytes 8388608
  1175.3 10.0 slice-start.2
  1175.3 11.2 slice-start.3
Sparse Core Ops, SparseCore 0:
  236.0 109.7 reduce-scatter.28
  349.5 106.8 reduce-scatter.26
  460.1 106.8 reduce-scatter.24
  570.6 106.8 reduce-scatter.22
  681.6 106.8 reduce-scatter.20
  792.6 106.8 reduce-scatter.18
  954.0 65.6 all-gather.13
  1022.5 66.6 all-gather.11
  1091.9 66.6 all-gather.9
where the time goes:
time: 1210 us; the launch traced here: 1200 us
  waiting for transfers between devices  700 us (58%)
  matrix products  312 us (26%)
  other arithmetic  85.3 us (7%)
  blocking collectives  46.3 us (4%)
  local copies, waits for them, and re-layouts  38.3 us (3%)
  between operations  17.2 us (1%)
    unnamed x15, waiting for transfers between devices  503 us
    reshape x3, waiting for transfers between devices, step(): t.reshape(-1, *t.shape[2:])  197 us
    dot_general x5, matrix products, layer(): up = jnp.dot(a, w['w_up'], preferred_element_type=jnp.float32)  114 us
    dot_general x5, matrix products, layer(): gate = jnp.dot(a, w['w_gate'], preferred_element_type=jnp.float32)  106 us
    dot_general x5, matrix products, matmul(): jnp.dot(a, w, preferred_element_type=jnp.float32).astype(jnp.bfloat16)  91.9 us
    unnamed x4, other arithmetic  63.6 us
    reduce_sum x1, blocking collectives, of_a_group(): jnp.sum(g * g)  46.3 us
    unnamed x37, local copies, waits for them, and re-layouts  38.3 us
  transfers between devices with their start and end apart: 9, of which 8 were waited for; matrix products, arithmetic and copies ran while one was open for 14% of the time, Pallas kernels for 0%

commit v1 on v0

v1 whole, which is shorter than its diff:
```python
import functools

import jax
import jax.numpy as jnp
from jax import lax
from jax.experimental import pallas as pl
from jax.experimental.pallas import tpu as pltpu
from jax.sharding import PartitionSpec as P

F32, BF16 = jnp.float32, jnp.bfloat16
MESH = pl.DeviceIdType.MESH
NT = (((1,), (1,)), ((), ()))
CHUNK = 512
PIECE = 2048
VMEM_LIMIT = 60 * 2**20


def dot(a, b):
    return jnp.dot(a, b, preferred_element_type=F32)


def dot_nt(a, b):
    return lax.dot_general(a, b, NT, preferred_element_type=F32)


def scale_of(wide):
    return lax.rsqrt(jnp.mean(wide * wide, -1, keepdims=True) + 1e-6)


def forward_kernel(steps, x_ref, wg_ref, wu_ref, wd_ref, h_ref, a_ref, acc_ref):
    f = pl.program_id(0)

    @pl.when(f == 0)
    def _():
        wide = x_ref[...].astype(F32)
        a_ref[...] = (wide * scale_of(wide)).astype(BF16)
        acc_ref[...] = jnp.zeros_like(acc_ref)

    a = a_ref[...]
    gate, up = dot(a, wg_ref[0]), dot(a, wu_ref[0])
    act = (gate * jax.nn.sigmoid(gate) * up).astype(BF16)
    acc_ref[...] += dot(act, wd_ref[0])

    @pl.when(f == steps - 1)
    def _():
        h_ref[...] = x_ref[...] + acc_ref[...].astype(BF16)


def forward(x, wg, wu, wd, number):
    (tokens, d), ff = x.shape, wg.shape[2]
    steps = ff // CHUNK
    whole = pl.BlockSpec((tokens, d), lambda f: (0, 0))
    return pl.pallas_call(
        functools.partial(forward_kernel, steps),
        name="layer_forward",
        grid=(steps,),
        out_shape=jax.ShapeDtypeStruct(x.shape, BF16),
        in_specs=[whole]
        + [pl.BlockSpec((1, d, CHUNK), lambda f: (number, 0, f))] * 2
        + [pl.BlockSpec((1, CHUNK, d), lambda f: (number, f, 0))],
        out_specs=whole,
        scratch_shapes=[pltpu.VMEM((tokens, d), BF16), pltpu.VMEM((tokens, d), F32)],
        compiler_params=pltpu.CompilerParams(vmem_limit_bytes=VMEM_LIMIT),
        cost_estimate=pl.CostEstimate(flops=6 * tokens * d * ff, bytes_accessed=6 * d * ff, transcendentals=0),
    )(x, wg, wu, wd)


def backward_kernel(steps, inner, h_ref, dy_ref, wg_ref, wu_ref, wd_ref, ggu_ref, gd_ref, *rest):
    if inner:
        dh_ref, a_ref, at_ref, dg_acc, du_acc = rest
    else:
        a_ref, at_ref = rest
    f = pl.program_id(0)

    @pl.when(f == 0)
    def _():
        wide = h_ref[...].astype(F32)
        a = (wide * scale_of(wide)).astype(BF16)
        a_ref[...] = a
        at_ref[...] = a.T
        if inner:
            dg_acc[...] = jnp.zeros_like(dg_acc)
            du_acc[...] = jnp.zeros_like(du_acc)

    a, dy = a_ref[...], dy_ref[...]
    gate, up = dot(a, wg_ref[0]), dot(a, wu_ref[0])
    dact = dot_nt(dy, wd_ref[0]).astype(BF16).astype(F32)
    sig = jax.nn.sigmoid(gate)
    silu = gate * sig
    act = (silu * up).astype(BF16)
    dup = (dact * silu).astype(BF16)
    dgate = (dact * up * (sig + silu * (1.0 - sig))).astype(BF16)
    if inner:
        dg_acc[...] += dot_nt(dgate, wg_ref[0])
        du_acc[...] += dot_nt(dup, wu_ref[0])
    at = at_ref[...]
    ggu_ref[0] = dot(at, dgate).astype(BF16).reshape(ggu_ref.shape[1:])
    ggu_ref[1] = dot(at, dup).astype(BF16).reshape(ggu_ref.shape[1:])
    dwd = lax.dot_general(act, dy, (((0,), (0,)), ((), ())), preferred_element_type=F32).astype(BF16)
    blocks, rows, columns = gd_ref.shape
    d = dwd.shape[1]
    for b in range(blocks):
        for k in range(columns // d):
            at_row = (b * (columns // d) + k) * rows
            gd_ref[b, :, k * d : (k + 1) * d] = dwd[at_row : at_row + rows]

    if inner:

        @pl.when(f == steps - 1)
        def _():
            da = (dg_acc[...].astype(BF16).astype(F32) + du_acc[...].astype(BF16).astype(F32)).astype(BF16).astype(F32)
            wide = h_ref[...].astype(F32)
            s = scale_of(wide)
            dot_ = jnp.mean(da * wide, -1, keepdims=True)
            dh = (da * s - wide * (s * s * s * dot_)).astype(BF16)
            dh_ref[...] = dy_ref[...] + dh


def backward(h, dy, wg, wu, wd, number, devices, inner):
    (tokens, d), ff = h.shape, wg.shape[2]
    steps, rows = ff // CHUNK, d // devices
    share = ff // devices
    whole = pl.BlockSpec((tokens, d), lambda f: (0, 0))
    outs = [jax.ShapeDtypeStruct((2, devices, rows, ff), BF16), jax.ShapeDtypeStruct((devices, rows, ff), BF16)]
    out_specs = [
        pl.BlockSpec((2, devices, rows, CHUNK), lambda f: (0, 0, 0, f)),
        pl.BlockSpec((CHUNK // share, rows, ff), lambda f: (f, 0, 0)),
    ]
    scratch = [pltpu.VMEM((tokens, d), BF16), pltpu.VMEM((d, tokens), BF16)]
    if inner:
        outs.append(jax.ShapeDtypeStruct((tokens, d), BF16))
        out_specs.append(whole)
        scratch += [pltpu.VMEM((tokens, d), F32)] * 2
    return pl.pallas_call(
        functools.partial(backward_kernel, steps, inner),
        name="layer_backward_inner" if inner else "layer_backward_first",
        grid=(steps,),
        out_shape=outs,
        in_specs=[whole, whole]
        + [pl.BlockSpec((1, d, CHUNK), lambda f: (number, 0, f))] * 2
        + [pl.BlockSpec((1, CHUNK, d), lambda f: (number, f, 0))],
        out_specs=out_specs,
        scratch_shapes=scratch,
        compiler_params=pltpu.CompilerParams(vmem_limit_bytes=VMEM_LIMIT),
        cost_estimate=pl.CostEstimate(
            flops=(16 if inner else 12) * tokens * d * ff, bytes_accessed=12 * d * ff, transcendentals=0
        ),
    )(h, dy, wg, wu, wd)


def wide_sum(*terms):
    total = terms[0].astype(F32)
    for t in terms[1:]:
        total = total + t.astype(F32)
    return total


def reduce_kernel(side, per_unit, g_refs, out_ref, sq_ref, S, r0, r1, r2, R, r3, r4, sqs, sqr,
                  load_sem, s0, v0, s1, v1, s2, v2, s3, v3, s4, v4, qs, qv):
    me = lax.axis_index("dp")
    core, chip = lax.rem(me, 2), lax.div(me, 2)
    y, x = lax.rem(chip, side), lax.div(chip, side)
    at = (x, y)

    def device(x, y, c):
        return {"dp": (x * side + y) * 2 + c}

    def step(axis, by):
        moved = lax.rem(at[axis] + by + side, side)
        return device(moved, y, core) if axis == 0 else device(x, moved, core)

    partner = device(x, y, 1 - core)
    neighbour = [[step(axis, 1), step(axis, -1)] for axis in (0, 1)]
    up = [lax.rem(at[axis] + 1, side) for axis in (0, 1)]
    down = [lax.rem(at[axis] + side - 1, side) for axis in (0, 1)]
    across = [lax.rem(at[axis] + 2, side) for axis in (0, 1)]
    piece = S.shape[-1]
    half = piece // 2
    quarter = half // 2
    units = out_ref.shape[0]
    N = units * per_unit

    barrier = pltpu.get_barrier_semaphore()
    for other in [partner] + neighbour[0] + neighbour[1]:
        pl.semaphore_signal(barrier, inc=1, device_id=other, device_id_type=MESH)
    pl.semaphore_wait(barrier, 5)

    def s_at(st, slot, p, lo=0, n=4):
        if st == 0:
            return S.at[slot, p, pl.ds(lo, n), :, pl.ds(0, half)]
        return S.at[slot, pl.ds(lo, n), p, :, pl.ds(half, half)]

    def remote(src, dst, ssem, rsem, to):
        return pltpu.make_async_remote_copy(
            src_ref=src, dst_ref=dst, send_sem=ssem, recv_sem=rsem, device_id=to, device_id_type=MESH
        )

    def columns(i):
        return pl.ds(pl.multiple_of(lax.rem(i, per_unit) * piece, piece), piece)

    def g_at(ref, index, i, c):
        if index is None:
            return ref.at[:, :, c, :, columns(i)]
        return ref.at[index, :, :, c, :, columns(i)]

    def load(ref, index, i, slot, par):
        return pltpu.make_async_copy(g_at(ref, index, i, core), S.at[slot], load_sem.at[par])

    def send0(ref, index, i, par):
        return remote(g_at(ref, index, i, 1 - core), r0.at[par], s0.at[par], v0.at[par], partner)

    def send1(st, d, slot, par):
        return remote(
            s_at(st, slot, across[st], 2 * d, 2), r1.at[par, st, d], s1.at[par, st, d], v1.at[par, st, d], neighbour[st][d]
        )

    def send2(st, d, slot, par):
        to = up[st] if d == 0 else down[st]
        return remote(s_at(st, slot, to), r2.at[par, st, d], s2.at[par, st, d], v2.at[par, st, d], neighbour[st][d])

    def send3(st, d, slot, par):
        o = 1 - st
        src = R.at[slot, st, across[o], :, pl.ds(d * quarter, quarter)]
        return remote(src, r3.at[par, st, d], s3.at[par, st, d], v3.at[par, st, d], neighbour[o][d])

    def send4(st, d, slot, par):
        o = 1 - st
        src = R.at[slot, st, up[o] if d == 0 else down[o]]
        return remote(src, r4.at[par, st, d], s4.at[par, st, d], v4.at[par, st, d], neighbour[o][d])

    BOTH = [(st, d) for st in (0, 1) for d in (0, 1)]
    sqs[0] = jnp.zeros(sqs.shape[1:], F32)

    def active(i):
        return jnp.logical_and(i >= 0, i < N)

    def body(t, carry):
        now, before = lax.rem(t, 2), lax.rem(t + 1, 2)

        def slot4(i):
            return lax.rem(i + 8, 4)

        i5 = t - 5

        @pl.when(active(i5))
        def _():
            slot = slot4(i5)
            for st in (0, 1):
                for d in (0, 1):
                    send4(st, d, slot, before).wait_recv()
                o = 1 - st
                total = wide_sum(R[slot, st, at[o]], r4[before, st, 0], r4[before, st, 1]).astype(BF16)
                where = pl.ds(pl.multiple_of(lax.rem(i5, per_unit) * piece + st * half, half), half)
                out_ref[lax.div(i5, per_unit), :, where] = total
                wide = total.astype(F32)
                square = (wide * wide).reshape(2, 8, half // 128, 128)
                sqs[0] += jnp.sum(jnp.sum(square, axis=2), axis=0)

        i4 = t - 4

        @pl.when(active(i4 - 2))
        def _():
            for st, d in BOTH:
                send4(st, d, slot4(i4 - 2), now).wait_send()

        @pl.when(active(i4))
        def _():
            slot = slot4(i4)
            for st, d in BOTH:
                send3(st, d, slot, before).wait_recv()
                o = 1 - st
                to, part = (up[o] if d == 0 else down[o]), pl.ds(d * quarter, quarter)
                R[slot, st, to, :, part] = wide_sum(R[slot, st, to, :, part], r3[before, st, d]).astype(BF16)
            for st, d in BOTH:
                send4(st, d, slot, now).start()

        i3 = t - 3

        @pl.when(active(i3 - 2))
        def _():
            for st, d in BOTH:
                send3(st, d, slot4(i3 - 2), now).wait_send()

        @pl.when(active(i3))
        def _():
            slot = slot4(i3)
            for st, d in BOTH:
                send2(st, d, slot, before).wait_recv()
            for st in (0, 1):
                for k in range(side):
                    mine = S[slot, at[0], k, :, :half] if st == 0 else S[slot, k, at[1], :, half:]
                    R[slot, st, k] = wide_sum(mine, r2[before, st, 0, k], r2[before, st, 1, k]).astype(BF16)
            for st, d in BOTH:
                send3(st, d, slot, now).start()

        i2 = t - 2

        @pl.when(active(i2 - 2))
        def _():
            for st, d in BOTH:
                send2(st, d, slot4(i2 - 2), now).wait_send()

        @pl.when(active(i2))
        def _():
            slot = slot4(i2)
            for st, d in BOTH:
                send1(st, d, slot, before).wait_recv()
                to = up[st] if d == 0 else down[st]
                for k in (2 * d, 2 * d + 1):
                    if st == 0:
                        S[slot, to, k, :, :half] = wide_sum(S[slot, to, k, :, :half], r1[before, st, d, k - 2 * d]).astype(BF16)
                    else:
                        S[slot, k, to, :, half:] = wide_sum(S[slot, k, to, :, half:], r1[before, st, d, k - 2 * d]).astype(BF16)
            for st, d in BOTH:
                send2(st, d, slot, now).start()

        i1 = t - 1

        @pl.when(active(i1 - 2))
        def _():
            for st, d in BOTH:
                send1(st, d, slot4(i1 - 2), now).wait_send()

        @pl.when(active(i1))
        def _():
            slot = slot4(i1)
            load(g_refs[1], None, i1, slot, before).wait()
            send0(g_refs[1], None, i1, before).wait_recv()

            def add(k, carry):
                kx, ky = lax.div(k, side), lax.rem(k, side)
                S[slot, kx, ky] = wide_sum(S[slot, kx, ky], r0[before, kx, ky]).astype(BF16)
                return carry

            lax.fori_loop(0, side * side, add, 0)
            for st, d in BOTH:
                send1(st, d, slot, now).start()

        @pl.when(active(t - 2))
        def _():
            send0(g_refs[1], None, t - 2, now).wait_send()

        for n, ref in enumerate(g_refs):
            first = 3 * (n // 2) + 2 * (n % 2)
            last = first + 2 - n % 2

            @pl.when(jnp.logical_and(t >= first * per_unit, t < last * per_unit))
            def _(ref=ref, first=first, n=n):
                index = lax.div(t, per_unit) - first if n % 2 == 0 else None
                load(ref, index, t, slot4(t), now).start()
                send0(ref, index, t, now).start()

        return carry

    lax.fori_loop(0, N + 6, body, 0)

    swaps = [partner]
    for axis in (0, 1):
        p = at[axis]
        for q in (p + 1 - 2 * lax.rem(p, 2), side - 1 - p):
            swaps.append(device(q, y, core) if axis == 0 else device(x, q, core))
    for n, other in enumerate(swaps):
        swap = remote(sqs.at[n], sqr.at[n], qs.at[n], qv.at[n], other)
        swap.start()
        swap.wait()
        sqs[n + 1] = sqs[n] + sqr[n]
    sq_ref[...] = sqs[len(swaps)]


def reduce_scatter(gradients, n):
    side = round((n // 2) ** 0.5)
    assert side == 4 and n == 2 * side * side
    rows, ff = gradients[0].shape[2:]
    flat = [
        g.reshape(2, side, side, 2, rows, ff) if g.ndim == 4 else g.reshape(side, side, 2, rows, ff) for g in gradients
    ]
    units = 3 * (len(flat) // 2)
    half = PIECE // 2
    dma = pltpu.SemaphoreType.DMA

    def kernel(*refs):
        reduce_kernel(side, ff // PIECE, refs[: len(flat)], *refs[len(flat) :])

    vmem = pl.BlockSpec(memory_space=pltpu.VMEM)
    return pl.pallas_call(
        kernel,
        name="reduce_gradients",
        out_shape=(jax.ShapeDtypeStruct((units, rows, ff), BF16), jax.ShapeDtypeStruct((8, 128), F32)),
        in_specs=[pl.BlockSpec(memory_space=pl.ANY)] * len(flat),
        out_specs=(vmem, vmem),
        scratch_shapes=[
            pltpu.VMEM((4, side, side, rows, PIECE), BF16),
            pltpu.VMEM((2, side, side, rows, PIECE), BF16),
            pltpu.VMEM((2, 2, 2, 2, rows, half), BF16),
            pltpu.VMEM((2, 2, 2, side, rows, half), BF16),
            pltpu.VMEM((4, 2, side, rows, half), BF16),
            pltpu.VMEM((2, 2, 2, rows, half // 2), BF16),
            pltpu.VMEM((2, 2, 2, rows, half), BF16),
            pltpu.VMEM((6, 8, 128), F32),
            pltpu.VMEM((5, 8, 128), F32),
            dma((2,)),
            dma((2,)),
            dma((2,)),
        ]
        + [dma((2, 2, 2))] * 8
        + [dma((5,))] * 2,
        compiler_params=pltpu.CompilerParams(collective_id=1, has_side_effects=True, vmem_limit_bytes=40 * 2**20),
        cost_estimate=pl.CostEstimate(flops=10**9, bytes_accessed=10**8, transcendentals=0),
    )(*flat)


def adamw(w, m, v, g):
    m = 0.9 * m + 0.1 * g
    v = 0.95 * v + 0.05 * g * g
    step = m * lax.rsqrt(v + 1e-8) + 0.1 * w
    return (w - 0.02 * step).astype(jnp.bfloat16), m, v


def solution(mesh):
    n = mesh.shape["dp"]

    def step(x, dy, *arrays):
        w, m, v = (arrays[i : i + 3] for i in (0, 3, 6))
        x, dy = x[0], dy[0]
        me = lax.axis_index("dp")
        h = forward(x, *w, 0)
        gu1, d1, dh = backward(h, dy, *w, 1, n, True)
        gu0, d0 = backward(x, dh, *w, 0, n, False)
        summed, squares = reduce_scatter([gu1, d1, gu0, d0], n)
        count = sum(t.size for t in w)
        factor = jnp.minimum(1.0, 0.5 * lax.rsqrt(jnp.sum(squares) / count + 1e-30))
        outs = []
        for k in range(3):
            rows = m[k].shape[1]
            g = jnp.stack([summed[3 + k], summed[k]])
            if k == 2:
                g = g.reshape(2, g.shape[1], -1, m[k].shape[2]).swapaxes(1, 2).reshape(m[k].shape)
            own = lax.dynamic_slice_in_dim(w[k], me * rows, rows, 1)
            outs.append(adamw(own.astype(F32), m[k], v[k], g.astype(F32) * factor))
        new = [lax.all_gather(one[0], "dp", axis=1, tiled=True) for one in outs]
        return (*new, *(one[1] for one in outs), *(one[2] for one in outs))

    seq, rep, own = P(("rep", "dp"), None, None), P(None, None, None), P(None, "dp", None)
    return jax.shard_map(
        step,
        mesh=mesh,
        in_specs=(seq, seq) + (rep,) * 3 + (own,) * 6,
        out_specs=(P("rep", None, None),) * 3 + (P("rep", "dp", None),) * 6,
        check_vma=False,
    )
```

time: 1210 us -> 649 us (0.54)
  waiting for transfers between devices: 700 us -> 201 us
  Pallas kernels: 0 us -> 381 us
  matrix products: 312 us -> 0 us
  other arithmetic: 85.3 us -> 11.9 us
  blocking collectives: 46.3 us -> 0 us
    unnamed x15 -> x3, waiting for transfers between devices: 503 us -> 0.16 us
    pallas_call x0 -> x4, Pallas kernels: none -> 381 us  [the longest x1 195 us: reduce_scatter(): pl.pallas_call(kernel, name='reduce_gradients', out_shape=(jax.ShapeDtype...]
    dot_general x15 -> x0, matrix products: 312 us -> none  [the longest x5 114 us: layer(): up = jnp.dot(a, w['w_up'], preferred_element_type=jnp.float32)]
    all_gather x0 -> x3, waiting for transfers between devices: none -> 201 us  [step(): new = [lax.all_gather(one[0], 'dp', axis=1, tiled=True) for one in outs]]
    reshape x3 -> x0, waiting for transfers between devices: 197 us -> none  [step(): t.reshape(-1, *t.shape[2:])]
    unnamed x4 -> x1, other arithmetic: 63.6 us -> 0.01 us
    reduce_sum x1 -> x0, blocking collectives: 46.3 us -> none  [of_a_group(): jnp.sum(g * g)]
    unnamed x37 -> x18, local copies, waits for them, and re-layouts: 38.3 us -> 38 us
  transfers between devices with their start and end apart: 9 -> 3, of which waited for: 8 -> 3; matrix products, arithmetic and copies ran while one was open for 14% -> 1% of each run, Pallas kernels for 0% -> 0%
where the time goes in v1:
time: 649 us
  Pallas kernels  381 us (59%)
  waiting for transfers between devices  201 us (31%)
  local copies, waits for them, and re-layouts  39.7 us (6%)
  between operations  14.5 us (2%)
  other arithmetic  11.9 us (2%)
    all_gather x3, waiting for transfers between devices, step(): new = [lax.all_gather(one[0], 'dp', axis=1, tiled=True) for one in outs]  201 us
    pallas_call x1, Pallas kernels, reduce_scatter(): pl.pallas_call(kernel, name='reduce_gradients', out_shape=(jax.ShapeDtype...  195 us
    pallas_call x2, Pallas kernels, backward(): pl.pallas_call(functools.partial(backward_kernel, steps, inner), name='la...  153 us
    unnamed x18, local copies, waits for them, and re-layouts  38 us
    pallas_call x1, Pallas kernels, forward(): pl.pallas_call(functools.partial(forward_kernel, steps), name='layer_forw...  32.7 us
  transfers between devices with their start and end apart: 3, of which 3 were waited for; matrix products, arithmetic and copies ran while one was open for 1% of the time, Pallas kernels for 0%

profile of v1, /device:TPU:97, one launch (start us, length us, event | category | flops | bytes accessed | tf_op | source)
XLA Modules:
  0.0 648.6 jit_solution(15797799511561686506)
XLA Ops:
  7.2 0.1 all-gather.8.cloned.1.call-start
  7.3 32.7 %layer_forward.1.h_ref = bf16[1024,512]{1,0:T(8,128)(2,1)} custom-call(bf16[1024,512]{1,0:T(8,128)(2,1)} %bitcast.30, bf16[2,512,8192]{2,1,0:T(8,128)(2,1)} %wg_ref.5, bf16[2,512,8192]{2,1,0:T(8,128)(2,1)} %wu_ref.5, bf16[2,8192,512]{2,1,0:T(8,128)(2,1)} %wd_ref.5), custom_call_target="tpu_custom_call" | custom-call | flops 25769803776 | bytes 25165824 | tf_op jit(solution)/shard_map/layer_forward/pallas_call | solution.py:53
  39.9 85.7 %layer_backward_inner.1 = (bf16[2,32,16,8192]{3,2,1,0:T(8,128)(2,1)}, bf16[32,16,8192]{2,1,0:T(8,128)(2,1)}, bf16[1024,512]{1,0:T(8,128)(2,1)}) custom-call(bf16[1024,512]{1,0:T(8,128)(2,1)} %layer_forward.1.h_ref, bf16[1024,512]{1,0:T(8,128)(2,1)} %bitcast.29, bf16[2,512,8192]{2,1,0:T(8,128)(2,1)} %wg_ref.5, bf16[2,512,8192]{2,1,0:T(8,128)(2,1)} %wu_ref.5, ...), custom_call_target="tpu_custom_call" | custom-call | flops 68719476736 | bytes 50331648 | tf_op jit(solution)/shard_map/layer_backward_inner/pallas_call | solution.py:134
  125.6 67.3 %layer_backward_first.1 = (bf16[2,32,16,8192]{3,2,1,0:T(8,128)(2,1)}, bf16[32,16,8192]{2,1,0:T(8,128)(2,1)}) custom-call(bf16[1024,512]{1,0:T(8,128)(2,1)} %bitcast.31, bf16[1024,512]{1,0:T(8,128)(2,1)} %get-tuple-element.18.dy_ref, bf16[2,512,8192]{2,1,0:T(8,128)(2,1)} %wg_ref.5, bf16[2,512,8192]{2,1,0:T(8,128)(2,1)} %wu_ref.5, bf16[2,8192,512]{2,1,0:T(8,128)(2,1)} %wd_ref.5), custom_call_target="tpu_custom_call" | custom-call | flops 51539607552 | bytes 50331648 | tf_op jit(solution)/shard_map/layer_backward_first/pallas_call | solution.py:134
  192.9 0.0 copy-start
  192.9 3.4 copy-done
  196.3 0.0 copy-start.2
  196.3 195.2 %reduce_gradients.1 = (bf16[6,16,8192]{2,1,0:T(8,128)(2,1)S(1)}, f32[8,128]{1,0:T(8,128)S(1)}) custom-call(bf16[2,4,4,2,16,8192]{5,4,3,2,1,0:T(8,128)(2,1)} %bitcast.22, bf16[4,4,2,16,8192]{4,3,2,1,0:T(8,128)(2,1)S(1)} %bitcast.21, bf16[2,4,4,2,16,8192]{5,4,3,2,1,0:T(8,128)(2,1)} %bitcast.23, bf16[4,4,2,16,8192]{4,3,2,1,0:T(8,128)(2,1)} %bitcast.26), custom_call_target="tpu_custom_call" | custom-call | flops 1000000000 | bytes 100000000 | tf_op jit(solution)/shard_map/reduce_gradients/pallas_call | solution.py:385
  391.5 0.6 reduce_sum.9
  392.8 0.9 fusion.17
  393.7 1.1 convert_multiply_fusion.3
  394.8 0.6 copy.21
  395.4 0.1 bitcast_bitcast_fusion
  395.5 0.6 copy.20
  396.1 0.0 copy-done.2
  396.1 3.2 fusion.8
  399.3 0.1 all-gather.8.cloned.1.call-update
  399.4 0.1 all-gather.6.cloned.1.call-start
  399.4 3.5 fusion.5
  403.0 0.1 all-gather.6.cloned.1.call-update
  403.0 0.1 all-gather.4.cloned.1.call-start
  403.1 3.5 fusion.2
  406.6 0.1 all-gather.4.cloned.1.call-update
  406.6 62.4 %all-gather.8.cloned.1.call-done = bf16[2,8192,512]{2,1,0:T(8,128)(2,1)} async-done(((bf16[2,256,512]{2,1,0:T(8,128)(2,1)}), bf16[2,8192,512]{2,1,0:T(8,128)(2,1)}) %all-gather.8.cloned.1.call-update) | async-done | bytes 16777232 | tf_op jit(solution)/shard_map/all_gather | solution.py:440
  469.1 69.4 %all-gather.6.cloned.1.call-done = bf16[2,512,8192]{2,1,0:T(8,128)(2,1)} async-done(((bf16[2,16,8192]{2,1,0:T(8,128)(2,1)}), bf16[2,512,8192]{2,1,0:T(8,128)(2,1)}) %all-gather.6.cloned.1.call-update) | async-done | bytes 16777232 | tf_op jit(solution)/shard_map/all_gather | solution.py:440
  538.5 69.5 %all-gather.4.cloned.1.call-done = bf16[2,512,8192]{2,1,0:T(8,128)(2,1)} async-done(((bf16[2,16,8192]{2,1,0:T(8,128)(2,1)}), bf16[2,512,8192]{2,1,0:T(8,128)(2,1)}) %all-gather.4.cloned.1.call-update) | async-done | bytes 16777232 | tf_op jit(solution)/shard_map/all_gather | solution.py:440
  608.0 0.0 copy-start.1
  608.0 0.0 slice-start
  608.0 0.0 slice-start.1
  608.0 16.7 %copy.25 = bf16[2,512,8192]{2,1,0:T(8,128)(2,1)} copy(bf16[2,512,8192]{2,1,0:T(8,128)(2,1)} %all-gather.4.cloned.1.call-done) | data formatting | bytes 33554432
  624.6 0.0 copy-done.1
  624.6 0.0 slice-start.2
  624.6 0.0 slice-start.3
  624.7 8.5 %copy.26 = bf16[2,512,8192]{2,1,0:T(8,128)(2,1)} copy(bf16[2,512,8192]{2,1,0:T(8,128)(2,1)S(1)} %copy-done.1) | data formatting | bytes 33554432
  633.2 0.0 slice-done
  633.2 0.0 slice-done.1
  633.2 1.5 slice-done.2
  634.7 1.2 slice-done.3
  635.9 6.2 copy.27
  (1 shorter events, 0.0 us)
Async XLA Ops:
  7.2 461.9 %all-gather.8.cloned.1.call-start = ((), (), s32[]{:S(2)}) async-start(), calls=%async_computation.2 | async-start | bytes 17301504 | tf_op jit(solution)/shard_map/all_gather | solution.py:440
  192.9 3.4 copy-start
  196.3 199.9 %copy-start.2 = (f32[2,256,512]{2,1,0:T(8,128)S(1)}, f32[2,256,512]{2,1,0:T(8,128)}, u32[]{:S(2)}) copy-start(f32[2,256,512]{2,1,0:T(8,128)} %param.21) | copy-start | bytes 3145732
  399.4 139.1 %all-gather.6.cloned.1.call-start = ((), (), s32[]{:S(2)}) async-start(), calls=%async_computation.1 | async-start | bytes 17301504 | tf_op jit(solution)/shard_map/all_gather | solution.py:440
  403.0 204.9 %all-gather.4.cloned.1.call-start = ((), (), s32[]{:S(2)}) async-start(), calls=%async_computation | async-start | bytes 17301504 | tf_op jit(solution)/shard_map/all_gather | solution.py:440
  608.0 16.7 %copy-start.1 = (bf16[2,512,8192]{2,1,0:T(8,128)(2,1)S(1)}, bf16[2,512,8192]{2,1,0:T(8,128)(2,1)}, u32[]{:S(2)}) copy-start(bf16[2,512,8192]{2,1,0:T(8,128)(2,1)} %all-gather.6.cloned.1.call-done) | copy-start | bytes 50331652
  608.0 25.2 %slice-start = ((s8[16777216]{0:T(1024)(128)(4,1)}), s8[4194304]{0:T(1024)(128)(4,1)S(1)}, s32[]{:S(2)}) async-start(s8[16777216]{0:T(1024)(128)(4,1)} %bitcast.24), calls=%async_computation.3 | async-start | bytes 8388608
  608.0 25.2 %slice-start.1 = ((s8[16777216]{0:T(1024)(128)(4,1)}), s8[4194304]{0:T(1024)(128)(4,1)S(1)}, s32[]{:S(2)}) async-start(s8[16777216]{0:T(1024)(128)(4,1)} %bitcast.24), calls=%async_computation.4 | async-start | bytes 8388608
  624.6 10.0 %slice-start.2 = ((s8[16777216]{0:T(1024)(128)(4,1)}), s8[4194304]{0:T(1024)(128)(4,1)S(1)}, s32[]{:S(2)}) async-start(s8[16777216]{0:T(1024)(128)(4,1)} %bitcast.24), calls=%async_computation.5 | async-start | bytes 8388608
  624.6 11.2 %slice-start.3 = ((s8[16777216]{0:T(1024)(128)(4,1)}), s8[4194304]{0:T(1024)(128)(4,1)S(1)}, s32[]{:S(2)}) async-start(s8[16777216]{0:T(1024)(128)(4,1)} %bitcast.24), calls=%async_computation.6 | async-start | bytes 8388608
Sparse Core Ops, SparseCore 0:
  399.5 69.5 all-gather.7
  471.8 66.6 all-gather.5
  541.2 66.6 all-gather.3

commit v2 on v0

v2 whole, which is shorter than its diff:
```python
import functools

import jax
import jax.numpy as jnp
from jax import lax
from jax.experimental import pallas as pl
from jax.experimental.pallas import tpu as pltpu
from jax.sharding import PartitionSpec as P

F32, BF16 = jnp.float32, jnp.bfloat16
MESH = pl.DeviceIdType.MESH
NT = (((1,), (1,)), ((), ()))
CHUNK = 512
VMEM_LIMIT = 60 * 2**20
GATHER_QUARTERS = 16


def dot(a, b):
    return jnp.dot(a, b, preferred_element_type=F32)


def dot_nt(a, b):
    return lax.dot_general(a, b, NT, preferred_element_type=F32)


def scale_of(wide):
    return lax.rsqrt(jnp.mean(wide * wide, -1, keepdims=True) + 1e-6)


def forward_kernel(steps, x_ref, wg_ref, wu_ref, wd_ref, h_ref, a_ref, acc_ref):
    f = pl.program_id(0)

    @pl.when(f == 0)
    def _():
        wide = x_ref[...].astype(F32)
        a_ref[...] = (wide * scale_of(wide)).astype(BF16)
        acc_ref[...] = jnp.zeros_like(acc_ref)

    a = a_ref[...]
    gate, up = dot(a, wg_ref[0]), dot(a, wu_ref[0])
    act = (gate * jax.nn.sigmoid(gate) * up).astype(BF16)
    acc_ref[...] += dot(act, wd_ref[0])

    @pl.when(f == steps - 1)
    def _():
        h_ref[...] = x_ref[...] + acc_ref[...].astype(BF16)


def forward(x, wg, wu, wd, number):
    (tokens, d), ff = x.shape, wg.shape[2]
    steps = ff // CHUNK
    whole = pl.BlockSpec((tokens, d), lambda f: (0, 0))
    return pl.pallas_call(
        functools.partial(forward_kernel, steps),
        name="layer_forward",
        grid=(steps,),
        out_shape=jax.ShapeDtypeStruct(x.shape, BF16),
        in_specs=[whole]
        + [pl.BlockSpec((1, d, CHUNK), lambda f: (number, 0, f))] * 2
        + [pl.BlockSpec((1, CHUNK, d), lambda f: (number, f, 0))],
        out_specs=whole,
        scratch_shapes=[pltpu.VMEM((tokens, d), BF16), pltpu.VMEM((tokens, d), F32)],
        compiler_params=pltpu.CompilerParams(vmem_limit_bytes=VMEM_LIMIT),
        cost_estimate=pl.CostEstimate(flops=6 * tokens * d * ff, bytes_accessed=6 * d * ff, transcendentals=0),
    )(x, wg, wu, wd)


def wide_sum(*terms):
    total = terms[0].astype(F32)
    for t in terms[1:]:
        total = total + t.astype(F32)
    return total


def remote(src, dst, ssem, rsem, to):
    return pltpu.make_async_remote_copy(
        src_ref=src, dst_ref=dst, send_sem=ssem, recv_sem=rsem, device_id=to, device_id_type=MESH
    )


class Torus:
    def __init__(self, side):
        me = lax.axis_index("dp")
        self.side = side
        self.core, chip = lax.rem(me, 2), lax.div(me, 2)
        self.at = (lax.div(chip, side), lax.rem(chip, side))
        self.partner = self.device(*self.at, 1 - self.core)
        self.up = [lax.rem(p + 1, side) for p in self.at]
        self.down = [lax.rem(p + side - 1, side) for p in self.at]
        self.across = [lax.rem(p + 2, side) for p in self.at]
        self.neighbour = [[self.along(axis, p[axis]) for p in (self.up, self.down)] for axis in (0, 1)]

    def device(self, x, y, c):
        return {"dp": (x * self.side + y) * 2 + c}

    def along(self, axis, p):
        return self.device(p, self.at[1], self.core) if axis == 0 else self.device(self.at[0], p, self.core)

    def next(self, axis, d):
        return self.up[axis] if d == 0 else self.down[axis]

    def greet(self):
        barrier = pltpu.get_barrier_semaphore()
        for other in [self.partner] + self.neighbour[0] + self.neighbour[1]:
            pl.semaphore_signal(barrier, inc=1, device_id=other, device_id_type=MESH)
        pl.semaphore_wait(barrier, 5)


BOTH = [(st, d) for st in (0, 1) for d in (0, 1)]


class Pipe:
    def __init__(self, torus, count, lag, sources, sink, scratch):
        self.torus, self.count, self.lag, self.sources, self.sink = torus, count, lag, sources, sink
        self.S, self.r0, self.r1, self.r2, self.R, self.r3, self.r4, self.s0, self.v0, *rest = scratch
        (self.s1, self.v1, self.s2, self.v2, self.s3, self.v3, self.s4, self.v4) = rest
        self.half = self.S.shape[-1] // 2

    @staticmethod
    def scratch(side, rows, width):
        half, dma = width // 2, pltpu.SemaphoreType.DMA
        return [
            pltpu.VMEM((4, side, side, rows, width), BF16),
            pltpu.VMEM((2, side, side, rows, width), BF16),
            pltpu.VMEM((2, 2, 2, 2, rows, half), BF16),
            pltpu.VMEM((2, 2, 2, side, rows, half), BF16),
            pltpu.VMEM((4, 2, side, rows, half), BF16),
            pltpu.VMEM((2, 2, 2, rows, half // 2), BF16),
            pltpu.VMEM((2, 2, 2, rows, half), BF16),
            dma((2,)),
            dma((2,)),
        ] + [dma((2, 2, 2))] * 8

    def s_at(self, st, slot, p, lo=0, n=4):
        if st == 0:
            return self.S.at[slot, p, pl.ds(lo, n), :, pl.ds(0, self.half)]
        return self.S.at[slot, pl.ds(lo, n), p, :, pl.ds(self.half, self.half)]

    def send0(self, view, par):
        return remote(view, self.r0.at[par], self.s0.at[par], self.v0.at[par], self.torus.partner)

    def any0(self, par):
        return self.send0(self.S.at[0], par)

    def send1(self, st, d, slot, par):
        src, k = self.s_at(st, slot, self.torus.across[st], 2 * d, 2), (par, st, d)
        return remote(src, self.r1.at[k], self.s1.at[k], self.v1.at[k], self.torus.neighbour[st][d])

    def send2(self, st, d, slot, par):
        src, k = self.s_at(st, slot, self.torus.next(st, d)), (par, st, d)
        return remote(src, self.r2.at[k], self.s2.at[k], self.v2.at[k], self.torus.neighbour[st][d])

    def send3(self, st, d, slot, par):
        o, k, quarter = 1 - st, (par, st, d), self.half // 2
        src = self.R.at[slot, st, self.torus.across[o], :, pl.ds(d * quarter, quarter)]
        return remote(src, self.r3.at[k], self.s3.at[k], self.v3.at[k], self.torus.neighbour[o][d])

    def send4(self, st, d, slot, par):
        o, k = 1 - st, (par, st, d)
        src = self.R.at[slot, st, self.torus.next(o, d)]
        return remote(src, self.r4.at[k], self.s4.at[k], self.v4.at[k], self.torus.neighbour[o][d])

    def active(self, i):
        return jnp.logical_and(i >= 0, i < self.count)

    def within(self, i, source):
        return jnp.logical_and(i >= source[0], i < source[1])

    def sent(self, i, send, now):
        @pl.when(self.active(i))
        def _():
            for st, d in BOTH:
                send(st, d, lax.rem(i + 8, 4), now).wait_send()

    def turn(self, t):
        torus, S, R, half = self.torus, self.S, self.R, self.half
        now, before = lax.rem(t, 2), lax.rem(t + 1, 2)
        i = t - self.lag

        def slot4(i):
            return lax.rem(i + 8, 4)

        @pl.when(self.active(i - 5))
        def _():
            slot = slot4(i - 5)
            for st in (0, 1):
                for d in (0, 1):
                    self.send4(st, d, slot, before).wait_recv()
                total = wide_sum(R[slot, st, torus.at[1 - st]], self.r4[before, st, 0], self.r4[before, st, 1])
                self.sink(i - 5, st, total.astype(BF16))

        self.sent(i - 6, self.send4, now)

        @pl.when(self.active(i - 4))
        def _():
            slot, quarter = slot4(i - 4), half // 2
            for st, d in BOTH:
                self.send3(st, d, slot, before).wait_recv()
                to, part = torus.next(1 - st, d), pl.ds(d * quarter, quarter)
                R[slot, st, to, :, part] = wide_sum(R[slot, st, to, :, part], self.r3[before, st, d]).astype(BF16)
            for st, d in BOTH:
                self.send4(st, d, slot, now).start()

        self.sent(i - 5, self.send3, now)

        @pl.when(self.active(i - 3))
        def _():
            slot = slot4(i - 3)
            for st, d in BOTH:
                self.send2(st, d, slot, before).wait_recv()
            for st in (0, 1):
                for k in range(torus.side):
                    mine = S[slot, torus.at[0], k, :, :half] if st == 0 else S[slot, k, torus.at[1], :, half:]
                    R[slot, st, k] = wide_sum(mine, self.r2[before, st, 0, k], self.r2[before, st, 1, k]).astype(BF16)
            for st, d in BOTH:
                self.send3(st, d, slot, now).start()

        self.sent(i - 4, self.send2, now)

        @pl.when(self.active(i - 2))
        def _():
            slot = slot4(i - 2)
            for st, d in BOTH:
                self.send1(st, d, slot, before).wait_recv()
                to = torus.next(st, d)
                for k in (0, 1):
                    arrived = self.r1[before, st, d, k]
                    if st == 0:
                        S[slot, to, 2 * d + k, :, :half] = wide_sum(S[slot, to, 2 * d + k, :, :half], arrived).astype(BF16)
                    else:
                        S[slot, 2 * d + k, to, :, half:] = wide_sum(S[slot, 2 * d + k, to, :, half:], arrived).astype(BF16)
            for st, d in BOTH:
                self.send2(st, d, slot, now).start()

        self.sent(i - 3, self.send1, now)

        @pl.when(self.active(i - 1))
        def _():
            self.any0(before).wait_recv()
            slot = slot4(i - 1)
            for source in self.sources:

                @pl.when(self.within(i - 1, source))
                def _(source=source):
                    def add(k, carry):
                        kx, ky = lax.div(k, torus.side), lax.rem(k, torus.side)
                        mine = source[2](i - 1, torus.core).at[kx, ky][...]
                        S[slot, kx, ky] = wide_sum(mine, self.r0[before, kx, ky]).astype(BF16)
                        return carry

                    lax.fori_loop(0, torus.side**2, add, 0)

            for st, d in BOTH:
                self.send1(st, d, slot, now).start()

        @pl.when(self.active(i - 2))
        def _():
            self.any0(now).wait_send()

        for source in self.sources:

            @pl.when(self.within(i, source))
            def _(source=source):
                self.send0(source[2](i, 1 - torus.core), now).start()


def gradient_kernel(
    side, ff, chunk, x_ref, h_ref, dy_ref, wg_hbm, wu_hbm, wd_hbm, out_ref, sq_ref,
    a_ref, at_ref, dy_now, dg_acc, du_acc, w_buf, w_sem, C, D, sqs, sqr, qs, qv, *pipes,
):
    torus = Torus(side)
    steps = ff // chunk
    rows, d = out_ref.shape[1], x_ref.shape[1]
    torus.greet()

    def set_input(ref):
        wide = ref[...].astype(F32)
        a = (wide * scale_of(wide)).astype(BF16)
        a_ref[...] = a
        at_ref[...] = a.T

    def loads(t, slot):
        number, f = 1 - lax.div(t, steps), lax.rem(t, steps)
        part = pl.ds(pl.multiple_of(f * chunk, chunk), chunk)
        return [
            pltpu.make_async_copy(wg_hbm.at[number, :, part], w_buf.at[slot, 0], w_sem.at[slot, 0]),
            pltpu.make_async_copy(wu_hbm.at[number, :, part], w_buf.at[slot, 1], w_sem.at[slot, 1]),
            pltpu.make_async_copy(wd_hbm.at[number, part, :], w_buf.at[slot, 2], w_sem.at[slot, 2]),
        ]

    for copy in loads(0, 0):
        copy.start()
    dy_now[...] = dy_ref[...]
    sqs[0] = jnp.zeros(sqs.shape[1:], F32)
    dg_acc[...] = jnp.zeros_like(dg_acc)
    du_acc[...] = jnp.zeros_like(du_acc)
    set_input(h_ref)

    def compute(t, inner):
        slot, c_slot = lax.rem(t, 2), lax.rem(t, C.shape[0])
        f = lax.rem(t, steps)
        a, dy = a_ref[...], dy_now[...]
        wg, wu, wd = (w_buf[slot, k] for k in range(3))
        gate, up = dot(a, wg), dot(a, wu)
        dact = dot_nt(dy, wd).astype(BF16).astype(F32)
        sig = jax.nn.sigmoid(gate)
        silu = gate * sig
        act = (silu * up).astype(BF16)
        dup = (dact * silu).astype(BF16)
        dgate = (dact * up * (sig + silu * (1.0 - sig))).astype(BF16)
        if inner:
            dg_acc[...] += dot_nt(dgate, wg)
            du_acc[...] += dot_nt(dup, wu)
        at = at_ref[...]
        C[c_slot, ..., :chunk] = dot(at, dgate).astype(BF16).reshape(side, side, 2, rows, chunk)
        C[c_slot, ..., chunk:] = dot(at, dup).astype(BF16).reshape(side, side, 2, rows, chunk)
        dwd = lax.dot_general(act, dy, (((0,), (0,)), ((), ())), preferred_element_type=F32).astype(BF16)
        pieces = ff // d
        for b in range(2):
            for k in range(pieces):
                row = (b * pieces + k) * rows
                D[1 if inner else 0, lax.div(f, side), lax.rem(f, side), b, :, k * d : (k + 1) * d] = dwd[row : row + rows]

    def squares(total):
        wide = total.astype(F32)
        sqs[0] += jnp.sum(jnp.sum((wide * wide).reshape(2, 8, -1, 128), axis=2), axis=0)

    def d_view(layer, first, width):
        def view(i, c):
            return D.at[layer, :, :, c, :, pl.ds(pl.multiple_of((i - first) * width, width), width)]

        return view

    def c_view(i, c):
        return C.at[lax.rem(i, C.shape[0]), :, :, c]

    def sink_main(i, st, total):
        squares(total)

        @pl.when(i < 2 * steps)
        def _():
            where = pl.ds(pl.multiple_of(lax.rem(i, steps) * chunk, chunk), chunk)
            out_ref[3 * lax.div(i, steps) + st, :, where] = total

        @pl.when(i >= 2 * steps)
        def _():
            where = pl.ds(pl.multiple_of((i - 2 * steps) * 2 * chunk + st * chunk, chunk), chunk)
            out_ref[5, :, where] = total

    def sink_down(i, st, total):
        squares(total)
        width = chunk // 2
        out_ref[2, :, pl.ds(pl.multiple_of(i * chunk + st * width, width), width)] = total

    tail = steps // 2
    n = len(pipes) // 2
    main = Pipe(
        torus, 2 * steps + tail, 1,
        [(0, 2 * steps, c_view), (2 * steps, 2 * steps + tail, d_view(0, 2 * steps, 2 * chunk))], sink_main, pipes[:n],
    )
    down = Pipe(torus, steps, steps + 1, [(0, steps, d_view(1, 0, chunk))], sink_down, pipes[n:])

    def body(t, carry):
        @pl.when(t == steps)
        def _():
            set_input(x_ref)

        main.turn(t)
        down.turn(t)

        @pl.when(t < 2 * steps)
        def _():
            @pl.when(t + 1 < 2 * steps)
            def _():
                for copy in loads(t + 1, lax.rem(t + 1, 2)):
                    copy.start()

            for copy in loads(t, lax.rem(t, 2)):
                copy.wait()

        @pl.when(t < steps)
        def _():
            compute(t, True)

        @pl.when(t == steps - 1)
        def _():
            da = (dg_acc[...].astype(BF16).astype(F32) + du_acc[...].astype(BF16).astype(F32)).astype(BF16).astype(F32)
            wide = h_ref[...].astype(F32)
            s = scale_of(wide)
            along = jnp.mean(da * wide, -1, keepdims=True)
            dy_now[...] = dy_ref[...] + (da * s - wide * (s * s * s * along)).astype(BF16)

        @pl.when(jnp.logical_and(t >= steps, t < 2 * steps))
        def _():
            compute(t, False)

        return carry

    lax.fori_loop(0, 2 * steps + tail + 7, body, 0)

    swaps = [torus.partner]
    for axis in (0, 1):
        p = torus.at[axis]
        for q in (p + 1 - 2 * lax.rem(p, 2), side - 1 - p):
            swaps.append(torus.along(axis, q))
    for k, other in enumerate(swaps):
        swap = remote(sqs.at[k], sqr.at[k], qs.at[k], qv.at[k], other)
        swap.start()
        swap.wait()
        sqs[k + 1] = sqs[k] + sqr[k]
    sq_ref[...] = sqs[len(swaps)]


def summed_gradients(x, h, dy, w, n):
    (tokens, d), ff = x.shape, w[0].shape[2]
    side = round((n // 2) ** 0.5)
    assert side == 4 and n == 2 * side * side and w[0].shape[0] == 2
    rows, chunk = d // n, CHUNK
    assert 2 * ff // n == chunk
    dma, vmem = pltpu.SemaphoreType.DMA, pl.BlockSpec(memory_space=pltpu.VMEM)
    return pl.pallas_call(
        functools.partial(gradient_kernel, side, ff, chunk),
        name="summed_gradients",
        out_shape=(jax.ShapeDtypeStruct((6, rows, ff), BF16), jax.ShapeDtypeStruct((8, 128), F32)),
        in_specs=[vmem] * 3 + [pl.BlockSpec(memory_space=pl.ANY)] * 3,
        out_specs=(vmem, vmem),
        scratch_shapes=[
            pltpu.VMEM((tokens, d), BF16),
            pltpu.VMEM((d, tokens), BF16),
            pltpu.VMEM((tokens, d), BF16),
            pltpu.VMEM((tokens, d), F32),
            pltpu.VMEM((tokens, d), F32),
            pltpu.VMEM((2, 3, d, chunk), BF16),
            dma((2, 3)),
            pltpu.VMEM((3, side, side, 2, rows, 2 * chunk), BF16),
            pltpu.VMEM((2, side, side, 2, rows, ff), BF16),
            pltpu.VMEM((6, 8, 128), F32),
            pltpu.VMEM((5, 8, 128), F32),
            dma((5,)),
            dma((5,)),
        ]
        + Pipe.scratch(side, rows, 2 * chunk)
        + Pipe.scratch(side, rows, chunk),
        compiler_params=pltpu.CompilerParams(collective_id=1, has_side_effects=True, vmem_limit_bytes=67043328),
        cost_estimate=pl.CostEstimate(flops=28 * tokens * d * ff, bytes_accessed=12 * d * ff, transcendentals=0),
    )(x, h, dy, *w)


def gather_kernel(
    side, own_gate, own_up, own_down, out_gate, out_up, out_down, own_sem, sa, va, sb, vb, sc, vc, sd, vd, se, ve
):
    torus = Torus(side)
    outs, owns = (out_gate, out_up, out_down), (own_gate, own_up, own_down)
    x, y = torus.at
    core = torus.core
    quarter = [ref.shape[-1] // GATHER_QUARTERS for ref in outs[:2]] + [out_down.shape[-2] // GATHER_QUARTERS]
    per_layer = GATHER_QUARTERS // 4
    layers = out_gate.shape[0]
    per_kind = layers * per_layer
    count = 3 * per_kind

    own_copies = [
        pltpu.make_async_copy(own, out.at[:, x, y, core], own_sem.at[k]) for k, (own, out) in enumerate(zip(owns, outs))
    ]
    for copy in own_copies:
        copy.start()
    torus.greet()
    for copy in own_copies:
        copy.wait()

    def part(kind, i, first, n):
        where = pl.ds(
            pl.multiple_of((lax.rem(i, per_layer) * 4 + first) * quarter[kind], quarter[kind]), n * quarter[kind]
        )
        return (slice(None), where) if kind < 2 else (where, slice(None))

    def layer_of(kind, i):
        return lax.div(i - kind * per_kind, per_layer)

    def place(kind, i, st, p, q, first, n):
        where = (p, q) if st == 0 else (q, p)
        return outs[kind].at[(layer_of(kind, i), *where, core, *part(kind, i, first, n))]

    ALL = slice(None)

    def send(src, dst, ss, vs, to):
        return remote(src, dst, ss, vs, to)

    def send_a(kind, i, st, d, par):
        dst = place(kind, i, st, torus.at[st], torus.at[1 - st], 2 * st, 2)
        src = owns[kind].at[(layer_of(kind, i), *part(kind, i, 2 * st, 2))]
        k = (par, st, d)
        return remote(src, dst, sa.at[k], va.at[k], torus.neighbour[1 - st][d])

    def send_b(kind, i, st, d, par):
        o = 1 - st
        ref, k = place(kind, i, st, torus.at[st], torus.next(o, 1 - d), 2 * st + d, 1), (par, st, d)
        return remote(ref, ref, sb.at[k], vb.at[k], torus.neighbour[o][d])

    def send_c(kind, i, st, d, par):
        ref, k = place(kind, i, st, torus.at[st], ALL, 2 * st, 2), (par, st, d)
        return remote(ref, ref, sc.at[k], vc.at[k], torus.neighbour[st][d])

    def send_d(kind, i, st, d, par):
        ref, k = place(kind, i, st, torus.next(st, 1 - d), pl.ds(2 * d, 2), 2 * st, 2), (par, st, d)
        return remote(ref, ref, sd.at[k], vd.at[k], torus.neighbour[st][d])

    def send_e(kind, i, par):
        ref = outs[kind].at[(layer_of(kind, i), ALL, ALL, core, *part(kind, i, 0, 4))]
        return remote(ref, ref, se.at[par], ve.at[par], torus.partner)

    def active(i):
        return jnp.logical_and(i >= 0, i < count)

    sends = [send_a, send_b, send_c, send_d]

    def body(t, carry):
        now, before = lax.rem(t, 2), lax.rem(t + 1, 2)

        @pl.when(active(t - 5))
        def _():
            send_e(0, 0, before).wait_recv()

        @pl.when(active(t - 6))
        def _():
            send_e(0, 0, now).wait_send()

        @pl.when(active(t - 4))
        def _():
            for st, d in BOTH:
                send_d(0, 0, st, d, before).wait_recv()
            for kind in range(3):

                @pl.when(lax.div(t - 4, per_kind) == kind)
                def _(kind=kind):
                    send_e(kind, t - 4, now).start()

        for s in (3, 2, 1, 0):

            @pl.when(active(t - s - 2))
            def _(s=s):
                for st, d in BOTH:
                    sends[s](0, 0, st, d, now).wait_send()

            @pl.when(active(t - s))
            def _(s=s):
                if s:
                    for st, d in BOTH:
                        sends[s - 1](0, 0, st, d, before).wait_recv()
                for kind in range(3):

                    @pl.when(lax.div(t - s, per_kind) == kind)
                    def _(kind=kind):
                        for st, d in BOTH:
                            sends[s](kind, t - s, st, d, now).start()

        return carry

    lax.fori_loop(0, count + 6, body, 0)


def gathered(blocks, n):
    side = round((n // 2) ** 0.5)
    assert side == 4 and n == 2 * side * side
    dma = pltpu.SemaphoreType.DMA
    whole = pl.pallas_call(
        functools.partial(gather_kernel, side),
        name="gather_weights",
        out_shape=[jax.ShapeDtypeStruct((b.shape[0], side, side, 2, *b.shape[1:]), b.dtype) for b in blocks],
        in_specs=[pl.BlockSpec(memory_space=pltpu.VMEM)] * 3,
        out_specs=[pl.BlockSpec(memory_space=pl.ANY)] * 3,
        scratch_shapes=[dma((3,))] + [dma((2, 2, 2))] * 8 + [dma((2,))] * 2,
        compiler_params=pltpu.CompilerParams(collective_id=2, has_side_effects=True, vmem_limit_bytes=16 * 2**20),
        cost_estimate=pl.CostEstimate(flops=10**8, bytes_accessed=10**8, transcendentals=0),
    )(*blocks)
    return [t.reshape(t.shape[0], -1, t.shape[-1]) for t in whole]


def adamw(w, m, v, g):
    m = 0.9 * m + 0.1 * g
    v = 0.95 * v + 0.05 * g * g
    step = m * lax.rsqrt(v + 1e-8) + 0.1 * w
    return (w - 0.02 * step).astype(jnp.bfloat16), m, v


def solution(mesh):
    n = mesh.shape["dp"]

    def step(x, dy, *arrays):
        w, m, v = (arrays[i : i + 3] for i in (0, 3, 6))
        x, dy = x[0], dy[0]
        me = lax.axis_index("dp")
        h = forward(x, *w, 0)
        summed, squares = summed_gradients(x, h, dy, w, n)
        count = sum(t.size for t in w)
        factor = jnp.minimum(1.0, 0.5 * lax.rsqrt(jnp.sum(squares) / count + 1e-30))
        outs = []
        for k in range(3):
            rows = m[k].shape[1]
            g = jnp.stack([summed[3 + k], summed[k]])
            if k == 2:
                g = g.reshape(2, g.shape[1], -1, m[k].shape[2]).swapaxes(1, 2).reshape(m[k].shape)
            own = lax.dynamic_slice_in_dim(w[k], me * rows, rows, 1)
            outs.append(adamw(own.astype(F32), m[k], v[k], g.astype(F32) * factor))
        new = gathered([one[0] for one in outs], n)
        return (*new, *(one[1] for one in outs), *(one[2] for one in outs))

    seq, rep, own = P(("rep", "dp"), None, None), P(None, None, None), P(None, "dp", None)
    return jax.shard_map(
        step,
        mesh=mesh,
        in_specs=(seq, seq) + (rep,) * 3 + (own,) * 6,
        out_specs=(P("rep", None, None),) * 3 + (P("rep", "dp", None),) * 6,
        check_vma=False,
    )
```

time: 1210 us -> 527 us (0.44)
  waiting for transfers between devices: 700 us -> 0 us
  Pallas kernels: 0 us -> 490 us
  matrix products: 312 us -> 0 us
  other arithmetic: 85.3 us -> 10.3 us
  blocking collectives: 46.3 us -> 0 us
  between operations: 17.2 us -> 1.4 us
  local copies, waits for them, and re-layouts: 38.3 us -> 25.7 us
    unnamed x15 -> x0, waiting for transfers between devices: 503 us -> none
    pallas_call x0 -> x3, Pallas kernels: none -> 490 us  [the longest x1 269 us: summed_gradients(): pl.pallas_call(functools.partial(gradient_kernel, side, ff, chunk), name=...]
    dot_general x15 -> x0, matrix products: 312 us -> none  [the longest x5 114 us: layer(): up = jnp.dot(a, w['w_up'], preferred_element_type=jnp.float32)]
    reshape x3 -> x0, waiting for transfers between devices: 197 us -> none  [step(): t.reshape(-1, *t.shape[2:])]
    unnamed x4 -> x1, other arithmetic: 63.6 us -> 0.01 us
    reduce_sum x1 -> x0, blocking collectives: 46.3 us -> none  [of_a_group(): jnp.sum(g * g)]
    unnamed x37 -> x11, local copies, waits for them, and re-layouts: 38.3 us -> 24.2 us
  transfers between devices with their start and end apart: 9 -> 0, of which waited for: 8 -> 0; matrix products, arithmetic and copies ran while one was open for 14% -> 0% of each run, Pallas kernels for 0% -> 0%
where the time goes in v2:
time: 527 us
  Pallas kernels  490 us (93%)
  local copies, waits for them, and re-layouts  25.7 us (5%)
  other arithmetic  10.3 us (2%)
    pallas_call x1, Pallas kernels, summed_gradients(): pl.pallas_call(functools.partial(gradient_kernel, side, ff, chunk), name=...  269 us
    pallas_call x1, Pallas kernels, gathered(): pl.pallas_call(functools.partial(gather_kernel, side), name='gather_weigh...  188 us
    pallas_call x1, Pallas kernels, forward(): pl.pallas_call(functools.partial(forward_kernel, steps), name='layer_forw...  32.7 us
    unnamed x11, local copies, waits for them, and re-layouts  24.2 us

profile of v2, /device:TPU:97, one launch (start us, length us, event | category | flops | bytes accessed | tf_op | source)
XLA Modules:
  0.0 527.2 jit_solution(9630342100450519498)
XLA Ops:
  0.6 32.7 %layer_forward.1.h_ref = bf16[1024,512]{1,0:T(8,128)(2,1)} custom-call(bf16[1024,512]{1,0:T(8,128)(2,1)} %bitcast.25, bf16[2,512,8192]{2,1,0:T(8,128)(2,1)} %wg_hbm.1, bf16[2,512,8192]{2,1,0:T(8,128)(2,1)} %wu_hbm.1, bf16[2,8192,512]{2,1,0:T(8,128)(2,1)} %wd_hbm.1), custom_call_target="tpu_custom_call" | custom-call | flops 25769803776 | bytes 25165824 | tf_op jit(solution)/shard_map/layer_forward/pallas_call | solution.py:53
  33.3 269.3 %summed_gradients.1 = (bf16[6,16,8192]{2,1,0:T(8,128)(2,1)}, f32[8,128]{1,0:T(8,128)}) custom-call(bf16[1024,512]{1,0:T(8,128)(2,1)} %bitcast.26, bf16[1024,512]{1,0:T(8,128)(2,1)} %layer_forward.1.h_ref, bf16[1024,512]{1,0:T(8,128)(2,1)} %bitcast.27, bf16[2,512,8192]{2,1,0:T(8,128)(2,1)} %wg_hbm.1, bf16[2,512,8192]{2,1,0:T(8,128)(2,1)} %wu_hbm.1, ...), custom_call_target="tpu_custom_call" | custom-call | flops 120259084288 | bytes 50331648 | tf_op jit(solution)/shard_map/summed_gradients/pallas_call | solution.py:421
  302.7 1.3 reduce_sum.9
  304.6 1.5 fusion.17
  306.1 0.1 convert_multiply_fusion.3
  306.2 0.1 copy.23
  306.3 3.6 fusion.8
  309.8 5.3 %fusion.2 = (bf16[2,16,8192]{2,1,0:T(8,128)(2,1)S(1)}, f32[2,16,8192]{2,1,0:T(8,128)}, f32[2,16,8192]{2,1,0:T(8,128)}, bf16[2,16,8192]{2,1,0:T(8,128)(2,1)S(1)},...) fusion(bf16[2,512,8192]{2,1,0:T(8,128)(2,1)} %wg_hbm.1, s32[]{:T(128)S(6)} %select_n.7, f32[]{:T(128)S(6)} %min_shard_map.3, ...), kind=kLoop, calls=%fused_computation.11 | loop fusion | flops 10485760 | bytes 11534344 | tf_op jit(solution)/shard_map/convert_element_type | solution.py:583
  315.2 187.8 %gather_weights.1 = (bf16[2,4,4,2,16,8192]{5,4,3,2,1,0:T(8,128)(2,1)S(1)}, bf16[2,4,4,2,16,8192]{5,4,3,2,1,0:T(8,128)(2,1)S(1)}, bf16[2,4,4,2,256,512]{5,4,3,2,1,0:T(8,128)(2,1)}) custom-call(bf16[2,16,8192]{2,1,0:T(8,128)(2,1)S(1)} %get-tuple-element.25.own_gate, bf16[2,16,8192]{2,1,0:T(8,128)(2,1)S(1)} %get-tuple-element.34.own_up, ...), custom_call_target="tpu_custom_call" | custom-call | flops 100000000 | bytes 100000000 | tf_op jit(solution)/shard_map/gather_weights/pallas_call | solution.py:566
  503.0 0.0 slice-start
  503.0 0.0 slice-start.1
  503.0 8.5 %copy.27 = bf16[2,512,8192]{2,1,0:T(8,128)(2,1)} copy(bf16[2,512,8192]{2,1,0:T(8,128)(2,1)S(1)} %bitcast.19) | data formatting | bytes 33554432
  511.5 0.0 slice-start.2
  511.5 0.0 slice-start.3
  511.5 8.4 %copy.28 = bf16[2,512,8192]{2,1,0:T(8,128)(2,1)} copy(bf16[2,512,8192]{2,1,0:T(8,128)(2,1)S(1)} %bitcast.18) | data formatting | bytes 33554432
  519.9 0.0 slice-done
  519.9 0.0 slice-done.1
  519.9 0.0 slice-done.2
  519.9 1.1 slice-done.3
  521.0 6.2 %copy.29 = bf16[2,8192,512]{2,1,0:T(8,128)(2,1)} copy(bf16[2,8192,512]{2,1,0:T(8,128)(2,1)S(1)} %bitcast.22) | data formatting | bytes 33554432
  (1 shorter events, 0.0 us)
Async XLA Ops:
  503.0 17.0 %slice-start = ((s8[16777216]{0:T(1024)(128)(4,1)}), s8[4194304]{0:T(1024)(128)(4,1)S(1)}, s32[]{:S(2)}) async-start(s8[16777216]{0:T(1024)(128)(4,1)} %bitcast.20), calls=%async_computation | async-start | bytes 8388608
  503.0 16.9 %slice-start.1 = ((s8[16777216]{0:T(1024)(128)(4,1)}), s8[4194304]{0:T(1024)(128)(4,1)S(1)}, s32[]{:S(2)}) async-start(s8[16777216]{0:T(1024)(128)(4,1)} %bitcast.20), calls=%async_computation.1 | async-start | bytes 8388608
  511.5 8.4 %slice-start.2 = ((s8[16777216]{0:T(1024)(128)(4,1)}), s8[4194304]{0:T(1024)(128)(4,1)S(1)}, s32[]{:S(2)}) async-start(s8[16777216]{0:T(1024)(128)(4,1)} %bitcast.20), calls=%async_computation.2 | async-start | bytes 8388608
  511.5 9.5 %slice-start.3 = ((s8[16777216]{0:T(1024)(128)(4,1)}), s8[4194304]{0:T(1024)(128)(4,1)S(1)}, s32[]{:S(2)}) async-start(s8[16777216]{0:T(1024)(128)(4,1)} %bitcast.20), calls=%async_computation.3 | async-start | bytes 8388608

commit v3 on v2

--- a/solution.py
+++ b/solution.py
@@ -11,6 +11,7 @@
 MESH = pl.DeviceIdType.MESH
 NT = (((1,), (1,)), ((), ()))
 CHUNK = 512
+FORWARD_CHUNK = 1024
 VMEM_LIMIT = 60 * 2**20
 GATHER_QUARTERS = 16
 
@@ -48,7 +49,7 @@
 
 def forward(x, wg, wu, wd, number):
     (tokens, d), ff = x.shape, wg.shape[2]
-    steps = ff // CHUNK
+    steps = ff // FORWARD_CHUNK
     whole = pl.BlockSpec((tokens, d), lambda f: (0, 0))
     return pl.pallas_call(
         functools.partial(forward_kernel, steps),
@@ -56,8 +57,8 @@
         grid=(steps,),
         out_shape=jax.ShapeDtypeStruct(x.shape, BF16),
         in_specs=[whole]
-        + [pl.BlockSpec((1, d, CHUNK), lambda f: (number, 0, f))] * 2
-        + [pl.BlockSpec((1, CHUNK, d), lambda f: (number, f, 0))],
+        + [pl.BlockSpec((1, d, FORWARD_CHUNK), lambda f: (number, 0, f))] * 2
+        + [pl.BlockSpec((1, FORWARD_CHUNK, d), lambda f: (number, f, 0))],
         out_specs=whole,
         scratch_shapes=[pltpu.VMEM((tokens, d), BF16), pltpu.VMEM((tokens, d), F32)],
         compiler_params=pltpu.CompilerParams(vmem_limit_bytes=VMEM_LIMIT),
@@ -120,16 +121,16 @@
     def scratch(side, rows, width):
         half, dma = width // 2, pltpu.SemaphoreType.DMA
         return [
+            pltpu.VMEM((6, side, side, rows, width), BF16),
             pltpu.VMEM((4, side, side, rows, width), BF16),
-            pltpu.VMEM((2, side, side, rows, width), BF16),
-            pltpu.VMEM((2, 2, 2, 2, rows, half), BF16),
-            pltpu.VMEM((2, 2, 2, side, rows, half), BF16),
-            pltpu.VMEM((4, 2, side, rows, half), BF16),
-            pltpu.VMEM((2, 2, 2, rows, half // 2), BF16),
-            pltpu.VMEM((2, 2, 2, rows, half), BF16),
-            dma((2,)),
-            dma((2,)),
-        ] + [dma((2, 2, 2))] * 8
+            pltpu.VMEM((4, 2, 2, 2, rows, half), BF16),
+            pltpu.VMEM((4, 2, 2, side, rows, half), BF16),
+            pltpu.VMEM((6, 2, side, rows, half), BF16),
+            pltpu.VMEM((4, 2, 2, rows, half // 2), BF16),
+            pltpu.VMEM((4, 2, 2, rows, half), BF16),
+            dma((4,)),
+            dma((4,)),
+        ] + [dma((4,))] * 8
 
     def s_at(self, st, slot, p, lo=0, n=4):
         if st == 0:
@@ -144,21 +145,25 @@
 
     def send1(self, st, d, slot, par):
         src, k = self.s_at(st, slot, self.torus.across[st], 2 * d, 2), (par, st, d)
-        return remote(src, self.r1.at[k], self.s1.at[k], self.v1.at[k], self.torus.neighbour[st][d])
+        return remote(src, self.r1.at[k], self.s1.at[par], self.v1.at[par], self.torus.neighbour[st][d])
 
     def send2(self, st, d, slot, par):
         src, k = self.s_at(st, slot, self.torus.next(st, d)), (par, st, d)
-        return remote(src, self.r2.at[k], self.s2.at[k], self.v2.at[k], self.torus.neighbour[st][d])
+        return remote(src, self.r2.at[k], self.s2.at[par], self.v2.at[par], self.torus.neighbour[st][d])
 
     def send3(self, st, d, slot, par):
         o, k, quarter = 1 - st, (par, st, d), self.half // 2
         src = self.R.at[slot, st, self.torus.across[o], :, pl.ds(d * quarter, quarter)]
-        return remote(src, self.r3.at[k], self.s3.at[k], self.v3.at[k], self.torus.neighbour[o][d])
+        return remote(src, self.r3.at[k], self.s3.at[par], self.v3.at[par], self.torus.neighbour[o][d])
 
     def send4(self, st, d, slot, par):
         o, k = 1 - st, (par, st, d)
         src = self.R.at[slot, st, self.torus.next(o, d)]
-        return remote(src, self.r4.at[k], self.s4.at[k], self.v4.at[k], self.torus.neighbour[o][d])
+        return remote(src, self.r4.at[k], self.s4.at[par], self.v4.at[par], self.torus.neighbour[o][d])
+
+    def all(self, n, par):
+        r, s, v = ((self.r1, self.s1, self.v1), (self.r2, self.s2, self.v2), (self.r3, self.s3, self.v3), (self.r4, self.s4, self.v4))[n - 1]
+        return remote(r.at[par], r.at[par], s.at[par], v.at[par], self.torus.partner)
 
     def active(self, i):
         return jnp.logical_and(i >= 0, i < self.count)
@@ -166,48 +171,45 @@
     def within(self, i, source):
         return jnp.logical_and(i >= source[0], i < source[1])
 
-    def sent(self, i, send, now):
+    def sent(self, i, n, now):
         @pl.when(self.active(i))
         def _():
-            for st, d in BOTH:
-                send(st, d, lax.rem(i + 8, 4), now).wait_send()
+            self.all(n, now).wait_send()
 
     def turn(self, t):
         torus, S, R, half = self.torus, self.S, self.R, self.half
-        now, before = lax.rem(t, 2), lax.rem(t + 1, 2)
+        now, before = lax.rem(t, 4), lax.rem(t + 2, 4)
         i = t - self.lag
 
-        def slot4(i):
-            return lax.rem(i + 8, 4)
-
-        @pl.when(self.active(i - 5))
-        def _():
-            slot = slot4(i - 5)
+        def slot6(i):
+            return lax.rem(i, 6)
+
+        @pl.when(self.active(i - 10))
+        def _():
+            slot = slot6(i - 10)
+            self.all(4, before).wait_recv()
             for st in (0, 1):
-                for d in (0, 1):
-                    self.send4(st, d, slot, before).wait_recv()
                 total = wide_sum(R[slot, st, torus.at[1 - st]], self.r4[before, st, 0], self.r4[before, st, 1])
-                self.sink(i - 5, st, total.astype(BF16))
-
-        self.sent(i - 6, self.send4, now)
-
-        @pl.when(self.active(i - 4))
-        def _():
-            slot, quarter = slot4(i - 4), half // 2
+                self.sink(i - 10, st, total.astype(BF16))
+
+        self.sent(i - 12, 4, now)
+
+        @pl.when(self.active(i - 8))
+        def _():
+            slot, quarter = slot6(i - 8), half // 2
+            self.all(3, before).wait_recv()
             for st, d in BOTH:
-                self.send3(st, d, slot, before).wait_recv()
                 to, part = torus.next(1 - st, d), pl.ds(d * quarter, quarter)
                 R[slot, st, to, :, part] = wide_sum(R[slot, st, to, :, part], self.r3[before, st, d]).astype(BF16)
             for st, d in BOTH:
                 self.send4(st, d, slot, now).start()
 
-        self.sent(i - 5, self.send3, now)
-
-        @pl.when(self.active(i - 3))
-        def _():
-            slot = slot4(i - 3)
-            for st, d in BOTH:
-                self.send2(st, d, slot, before).wait_recv()
+        self.sent(i - 10, 3, now)
+
+        @pl.when(self.active(i - 6))
+        def _():
+            slot = slot6(i - 6)
+            self.all(2, before).wait_recv()
             for st in (0, 1):
                 for k in range(torus.side):
                     mine = S[slot, torus.at[0], k, :, :half] if st == 0 else S[slot, k, torus.at[1], :, half:]
@@ -215,13 +217,13 @@
             for st, d in BOTH:
                 self.send3(st, d, slot, now).start()
 
-        self.sent(i - 4, self.send2, now)
-
-        @pl.when(self.active(i - 2))
-        def _():
-            slot = slot4(i - 2)
+        self.sent(i - 8, 2, now)
+
+        @pl.when(self.active(i - 4))
+        def _():
+            slot = slot6(i - 4)
+            self.all(1, before).wait_recv()
             for st, d in BOTH:
-                self.send1(st, d, slot, before).wait_recv()
                 to = torus.next(st, d)
                 for k in (0, 1):
                     arrived = self.r1[before, st, d, k]
@@ -232,30 +234,30 @@
             for st, d in BOTH:
                 self.send2(st, d, slot, now).start()
 
-        self.sent(i - 3, self.send1, now)
-
-        @pl.when(self.active(i - 1))
+        self.sent(i - 6, 1, now)
+
+        @pl.when(self.active(i - 2))
         def _():
             self.any0(before).wait_recv()
-            slot = slot4(i - 1)
+            slot = slot6(i - 2)
             for source in self.sources:
 
-                @pl.when(self.within(i - 1, source))
+                @pl.when(self.within(i - 2, source))
                 def _(source=source):
                     def add(k, carry):
                         kx, ky = lax.div(k, torus.side), lax.rem(k, torus.side)
-                        mine = source[2](i - 1, torus.core).at[kx, ky][...]
+                        mine = source[2](i - 2, torus.core).at[kx, ky][...]
                         S[slot, kx, ky] = wide_sum(mine, self.r0[before, kx, ky]).astype(BF16)
                         return carry
 
-                    lax.fori_loop(0, torus.side**2, add, 0)
+                    lax.fori_loop(0, torus.side**2, add, 0, unroll=4)
 
             for st, d in BOTH:
                 self.send1(st, d, slot, now).start()
 
         @pl.when(self.active(i - 2))
         def _():
-            self.any0(now).wait_send()
+            self.any0(before).wait_send()
 
         for source in self.sources:
 
@@ -265,7 +267,7 @@
 
 
 def gradient_kernel(
-    side, ff, chunk, x_ref, h_ref, dy_ref, wg_hbm, wu_hbm, wd_hbm, out_ref, sq_ref,
+    side, ff, chunk, count, x_ref, h_ref, dy_ref, wg_hbm, wu_hbm, wd_hbm, out_ref, factor_ref,
     a_ref, at_ref, dy_now, dg_acc, du_acc, w_buf, w_sem, C, D, sqs, sqr, qs, qv, *pipes,
 ):
     torus = Torus(side)
@@ -396,7 +398,7 @@
 
         return carry
 
-    lax.fori_loop(0, 2 * steps + tail + 7, body, 0)
+    lax.fori_loop(0, 2 * steps + tail + 13, body, 0)
 
     swaps = [torus.partner]
     for axis in (0, 1):
@@ -408,7 +410,8 @@
         swap.start()
         swap.wait()
         sqs[k + 1] = sqs[k] + sqr[k]
-    sq_ref[...] = sqs[len(swaps)]
+    total = jnp.broadcast_to(jnp.sum(sqs[len(swaps)], keepdims=True), factor_ref.shape)
+    factor_ref[...] = jnp.minimum(1.0, 0.5 * lax.rsqrt(total / count + 1e-30))
 
 
 def summed_gradients(x, h, dy, w, n):
@@ -419,7 +422,7 @@
     assert 2 * ff // n == chunk
     dma, vmem = pltpu.SemaphoreType.DMA, pl.BlockSpec(memory_space=pltpu.VMEM)
     return pl.pallas_call(
-        functools.partial(gradient_kernel, side, ff, chunk),
+        functools.partial(gradient_kernel, side, ff, chunk, sum(t.size for t in w)),
         name="summed_gradients",
         out_shape=(jax.ShapeDtypeStruct((6, rows, ff), BF16), jax.ShapeDtypeStruct((8, 128), F32)),
         in_specs=[vmem] * 3 + [pl.BlockSpec(memory_space=pl.ANY)] * 3,
@@ -483,9 +486,6 @@
 
     ALL = slice(None)
 
-    def send(src, dst, ss, vs, to):
-        return remote(src, dst, ss, vs, to)
-
     def send_a(kind, i, st, d, par):
         dst = place(kind, i, st, torus.at[st], torus.at[1 - st], 2 * st, 2)
         src = owns[kind].at[(layer_of(kind, i), *part(kind, i, 2 * st, 2))]
@@ -515,48 +515,48 @@
     sends = [send_a, send_b, send_c, send_d]
 
     def body(t, carry):
-        now, before = lax.rem(t, 2), lax.rem(t + 1, 2)
-
-        @pl.when(active(t - 5))
+        now, before = lax.rem(t, 4), lax.rem(t + 2, 4)
+
+        @pl.when(active(t - 10))
         def _():
             send_e(0, 0, before).wait_recv()
 
-        @pl.when(active(t - 6))
+        @pl.when(active(t - 12))
         def _():
             send_e(0, 0, now).wait_send()
 
-        @pl.when(active(t - 4))
+        @pl.when(active(t - 8))
         def _():
             for st, d in BOTH:
                 send_d(0, 0, st, d, before).wait_recv()
             for kind in range(3):
 
-                @pl.when(lax.div(t - 4, per_kind) == kind)
+                @pl.when(lax.div(t - 8, per_kind) == kind)
                 def _(kind=kind):
-                    send_e(kind, t - 4, now).start()
+                    send_e(kind, t - 8, now).start()
 
         for s in (3, 2, 1, 0):
 
-            @pl.when(active(t - s - 2))
+            @pl.when(active(t - 2 * s - 4))
             def _(s=s):
                 for st, d in BOTH:
                     sends[s](0, 0, st, d, now).wait_send()
 
-            @pl.when(active(t - s))
+            @pl.when(active(t - 2 * s))
             def _(s=s):
                 if s:
                     for st, d in BOTH:
                         sends[s - 1](0, 0, st, d, before).wait_recv()
                 for kind in range(3):
 
-                    @pl.when(lax.div(t - s, per_kind) == kind)
+                    @pl.when(lax.div(t - 2 * s, per_kind) == kind)
                     def _(kind=kind):
                         for st, d in BOTH:
-                            sends[s](kind, t - s, st, d, now).start()
+                            sends[s](kind, t - 2 * s, st, d, now).start()
 
         return carry
 
-    lax.fori_loop(0, count + 6, body, 0)
+    lax.fori_loop(0, count + 12, body, 0)
 
 
 def gathered(blocks, n):
@@ -569,7 +569,7 @@
         out_shape=[jax.ShapeDtypeStruct((b.shape[0], side, side, 2, *b.shape[1:]), b.dtype) for b in blocks],
         in_specs=[pl.BlockSpec(memory_space=pltpu.VMEM)] * 3,
         out_specs=[pl.BlockSpec(memory_space=pl.ANY)] * 3,
-        scratch_shapes=[dma((3,))] + [dma((2, 2, 2))] * 8 + [dma((2,))] * 2,
+        scratch_shapes=[dma((3,))] + [dma((4, 2, 2))] * 8 + [dma((4,))] * 2,
         compiler_params=pltpu.CompilerParams(collective_id=2, has_side_effects=True, vmem_limit_bytes=16 * 2**20),
         cost_estimate=pl.CostEstimate(flops=10**8, bytes_accessed=10**8, transcendentals=0),
     )(*blocks)
@@ -591,9 +591,8 @@
         x, dy = x[0], dy[0]
         me = lax.axis_index("dp")
         h = forward(x, *w, 0)
-        summed, squares = summed_gradients(x, h, dy, w, n)
-        count = sum(t.size for t in w)
-        factor = jnp.minimum(1.0, 0.5 * lax.rsqrt(jnp.sum(squares) / count + 1e-30))
+        summed, factor = summed_gradients(x, h, dy, w, n)
+        factor = factor[0, 0]
         outs = []
         for k in range(3):
             rows = m[k].shape[1]

time: 527 us -> 459 us (0.87)
  Pallas kernels: 490 us -> 421 us
    pallas_call x1, Pallas kernels: 188 us -> 141 us  [gathered(): pl.pallas_call(functools.partial(gather_kernel, side), name='gather_weigh...]
    pallas_call x1, Pallas kernels: 269 us -> 248 us  [summed_gradients(): pl.pallas_call(functools.partial(gradient_kernel, side, ff, chunk, sum((t...]
where the time goes in v3:
time: 459 us
  Pallas kernels  421 us (92%)
  local copies, waits for them, and re-layouts  26.9 us (6%)
  other arithmetic  10.3 us (2%)
    pallas_call x1, Pallas kernels, summed_gradients(): pl.pallas_call(functools.partial(gradient_kernel, side, ff, chunk, sum((t...  248 us
    pallas_call x1, Pallas kernels, gathered(): pl.pallas_call(functools.partial(gather_kernel, side), name='gather_weigh...  141 us
    pallas_call x1, Pallas kernels, forward(): pl.pallas_call(functools.partial(forward_kernel, steps), name='layer_forw...  31.8 us
    unnamed x11, local copies, waits for them, and re-layouts  24.2 us
    convert_element_type x2, other arithmetic, adamw(): return ((w - 0.02 * step).astype(jnp.bfloat16), m, v)  9.58 us

profile of v3, /device:TPU:97, one launch (start us, length us, event | category | flops | bytes accessed | tf_op | source)
XLA Modules:
  0.0 458.9 jit_solution(2524794525619392527)
XLA Ops:
  0.6 31.8 %layer_forward.1.h_ref = bf16[1024,512]{1,0:T(8,128)(2,1)} custom-call(bf16[1024,512]{1,0:T(8,128)(2,1)} %bitcast.26, bf16[2,512,8192]{2,1,0:T(8,128)(2,1)} %wg_hbm.1, bf16[2,512,8192]{2,1,0:T(8,128)(2,1)} %wu_hbm.1, bf16[2,8192,512]{2,1,0:T(8,128)(2,1)} %wd_hbm.1), custom_call_target="tpu_custom_call" | custom-call | flops 25769803776 | bytes 25165824 | tf_op jit(solution)/shard_map/layer_forward/pallas_call | solution.py:54
  32.4 247.7 %summed_gradients.1 = (bf16[6,16,8192]{2,1,0:T(8,128)(2,1)}, f32[8,128]{1,0:T(8,128)}) custom-call(bf16[1024,512]{1,0:T(8,128)(2,1)} %bitcast.27, bf16[1024,512]{1,0:T(8,128)(2,1)} %layer_forward.1.h_ref, bf16[1024,512]{1,0:T(8,128)(2,1)} %bitcast.28, bf16[2,512,8192]{2,1,0:T(8,128)(2,1)} %wg_hbm.1, bf16[2,512,8192]{2,1,0:T(8,128)(2,1)} %wu_hbm.1, ...), custom_call_target="tpu_custom_call" | custom-call | flops 120259084288 | bytes 50331648 | tf_op jit(solution)/shard_map/summed_gradients/pallas_call | solution.py:424
  280.1 1.2 slice.23
  281.3 1.4 fusion.17
  282.8 0.7 convert_multiply_fusion.3
  283.5 0.1 copy.23
  283.6 3.6 fusion.8
  287.2 6.0 %fusion.2 = (bf16[2,16,8192]{2,1,0:T(8,128)(2,1)S(1)}, f32[2,16,8192]{2,1,0:T(8,128)}, f32[2,16,8192]{2,1,0:T(8,128)}, bf16[2,16,8192]{2,1,0:T(8,128)(2,1)S(1)},...) fusion(bf16[2,512,8192]{2,1,0:T(8,128)(2,1)} %wg_hbm.1, s32[]{:T(128)S(6)} %select_n.7, f32[]{:T(128)} %bitcast.2, ...), kind=kLoop, calls=%fused_computation.11 | loop fusion | flops 10485760 | bytes 11534344 | tf_op jit(solution)/shard_map/convert_element_type | solution.py:583
  293.2 141.5 %gather_weights.1 = (bf16[2,4,4,2,16,8192]{5,4,3,2,1,0:T(8,128)(2,1)S(1)}, bf16[2,4,4,2,16,8192]{5,4,3,2,1,0:T(8,128)(2,1)S(1)}, bf16[2,4,4,2,256,512]{5,4,3,2,1,0:T(8,128)(2,1)}) custom-call(bf16[2,16,8192]{2,1,0:T(8,128)(2,1)S(1)} %get-tuple-element.25.own_gate, bf16[2,16,8192]{2,1,0:T(8,128)(2,1)S(1)} %get-tuple-element.34.own_up, ...), custom_call_target="tpu_custom_call" | custom-call | flops 100000000 | bytes 100000000 | tf_op jit(solution)/shard_map/gather_weights/pallas_call | solution.py:566
  434.7 0.0 slice-start
  434.7 0.0 slice-start.1
  434.7 8.5 %copy.27 = bf16[2,512,8192]{2,1,0:T(8,128)(2,1)} copy(bf16[2,512,8192]{2,1,0:T(8,128)(2,1)S(1)} %bitcast.20) | data formatting | bytes 33554432
  443.2 0.0 slice-start.2
  443.2 0.0 slice-start.3
  443.2 8.4 %copy.28 = bf16[2,512,8192]{2,1,0:T(8,128)(2,1)} copy(bf16[2,512,8192]{2,1,0:T(8,128)(2,1)S(1)} %bitcast.19) | data formatting | bytes 33554432
  451.6 0.0 slice-done
  451.6 0.0 slice-done.1
  451.6 0.0 slice-done.2
  451.6 1.1 slice-done.3
  452.7 6.2 %copy.29 = bf16[2,8192,512]{2,1,0:T(8,128)(2,1)} copy(bf16[2,8192,512]{2,1,0:T(8,128)(2,1)S(1)} %bitcast.23) | data formatting | bytes 33554432
  (1 shorter events, 0.0 us)
Async XLA Ops:
  434.7 17.0 %slice-start = ((s8[16777216]{0:T(1024)(128)(4,1)}), s8[4194304]{0:T(1024)(128)(4,1)S(1)}, s32[]{:S(2)}) async-start(s8[16777216]{0:T(1024)(128)(4,1)} %bitcast.21), calls=%async_computation | async-start | bytes 8388608
  434.7 16.9 %slice-start.1 = ((s8[16777216]{0:T(1024)(128)(4,1)}), s8[4194304]{0:T(1024)(128)(4,1)S(1)}, s32[]{:S(2)}) async-start(s8[16777216]{0:T(1024)(128)(4,1)} %bitcast.21), calls=%async_computation.1 | async-start | bytes 8388608
  443.2 8.4 %slice-start.2 = ((s8[16777216]{0:T(1024)(128)(4,1)}), s8[4194304]{0:T(1024)(128)(4,1)S(1)}, s32[]{:S(2)}) async-start(s8[16777216]{0:T(1024)(128)(4,1)} %bitcast.21), calls=%async_computation.2 | async-start | bytes 8388608
  443.2 9.5 %slice-start.3 = ((s8[16777216]{0:T(1024)(128)(4,1)}), s8[4194304]{0:T(1024)(128)(4,1)S(1)}, s32[]{:S(2)}) async-start(s8[16777216]{0:T(1024)(128)(4,1)} %bitcast.21), calls=%async_computation.3 | async-start | bytes 8388608

commit v4 on v3

--- a/solution.py
+++ b/solution.py
@@ -89,6 +89,7 @@
         self.up = [lax.rem(p + 1, side) for p in self.at]
         self.down = [lax.rem(p + side - 1, side) for p in self.at]
         self.across = [lax.rem(p + 2, side) for p in self.at]
+        self.far = [self.along(axis, self.across[axis]) for axis in (0, 1)]
         self.neighbour = [[self.along(axis, p[axis]) for p in (self.up, self.down)] for axis in (0, 1)]
 
     def device(self, x, y, c):
@@ -100,11 +101,11 @@
     def next(self, axis, d):
         return self.up[axis] if d == 0 else self.down[axis]
 
-    def greet(self):
+    def greet(self, *more):
         barrier = pltpu.get_barrier_semaphore()
-        for other in [self.partner] + self.neighbour[0] + self.neighbour[1]:
+        for other in [self.partner, *self.neighbour[0], *self.neighbour[1], *more]:
             pl.semaphore_signal(barrier, inc=1, device_id=other, device_id_type=MESH)
-        pl.semaphore_wait(barrier, 5)
+        pl.semaphore_wait(barrier, 5 + len(more))
 
 
 BOTH = [(st, d) for st in (0, 1) for d in (0, 1)]
@@ -115,13 +116,13 @@
         self.torus, self.count, self.lag, self.sources, self.sink = torus, count, lag, sources, sink
         self.S, self.r0, self.r1, self.r2, self.R, self.r3, self.r4, self.s0, self.v0, *rest = scratch
         (self.s1, self.v1, self.s2, self.v2, self.s3, self.v3, self.s4, self.v4) = rest
-        self.half = self.S.shape[-1] // 2
+        self.half = self.S.shape[-1]
 
     @staticmethod
     def scratch(side, rows, width):
         half, dma = width // 2, pltpu.SemaphoreType.DMA
         return [
-            pltpu.VMEM((6, side, side, rows, width), BF16),
+            pltpu.VMEM((6, 2, side, side, rows, half), BF16),
             pltpu.VMEM((4, side, side, rows, width), BF16),
             pltpu.VMEM((4, 2, 2, 2, rows, half), BF16),
             pltpu.VMEM((4, 2, 2, side, rows, half), BF16),
@@ -133,15 +134,13 @@
         ] + [dma((4,))] * 8
 
     def s_at(self, st, slot, p, lo=0, n=4):
-        if st == 0:
-            return self.S.at[slot, p, pl.ds(lo, n), :, pl.ds(0, self.half)]
-        return self.S.at[slot, pl.ds(lo, n), p, :, pl.ds(self.half, self.half)]
+        return self.S.at[slot, st, p, pl.ds(lo, n)]
 
     def send0(self, view, par):
         return remote(view, self.r0.at[par], self.s0.at[par], self.v0.at[par], self.torus.partner)
 
     def any0(self, par):
-        return self.send0(self.S.at[0], par)
+        return self.send0(self.r0.at[par], par)
 
     def send1(self, st, d, slot, par):
         src, k = self.s_at(st, slot, self.torus.across[st], 2 * d, 2), (par, st, d)
@@ -212,8 +211,7 @@
             self.all(2, before).wait_recv()
             for st in (0, 1):
                 for k in range(torus.side):
-                    mine = S[slot, torus.at[0], k, :, :half] if st == 0 else S[slot, k, torus.at[1], :, half:]
-                    R[slot, st, k] = wide_sum(mine, self.r2[before, st, 0, k], self.r2[before, st, 1, k]).astype(BF16)
+                    R[slot, st, k] = wide_sum(S[slot, st, torus.at[st], k], self.r2[before, st, 0, k], self.r2[before, st, 1, k]).astype(BF16)
             for st, d in BOTH:
                 self.send3(st, d, slot, now).start()
 
@@ -226,11 +224,7 @@
             for st, d in BOTH:
                 to = torus.next(st, d)
                 for k in (0, 1):
-                    arrived = self.r1[before, st, d, k]
-                    if st == 0:
-                        S[slot, to, 2 * d + k, :, :half] = wide_sum(S[slot, to, 2 * d + k, :, :half], arrived).astype(BF16)
-                    else:
-                        S[slot, 2 * d + k, to, :, half:] = wide_sum(S[slot, 2 * d + k, to, :, half:], arrived).astype(BF16)
+                    S[slot, st, to, 2 * d + k] = wide_sum(S[slot, st, to, 2 * d + k], self.r1[before, st, d, k]).astype(BF16)
             for st, d in BOTH:
                 self.send2(st, d, slot, now).start()
 
@@ -247,7 +241,8 @@
                     def add(k, carry):
                         kx, ky = lax.div(k, torus.side), lax.rem(k, torus.side)
                         mine = source[2](i - 2, torus.core).at[kx, ky][...]
-                        S[slot, kx, ky] = wide_sum(mine, self.r0[before, kx, ky]).astype(BF16)
+                        both = wide_sum(mine, self.r0[before, kx, ky]).astype(BF16)
+                        S[slot, 0, kx, ky], S[slot, 1, ky, kx] = both[:, :half], both[:, half:]
                         return carry
 
                     lax.fori_loop(0, torus.side**2, add, 0, unroll=4)
@@ -273,7 +268,7 @@
     torus = Torus(side)
     steps = ff // chunk
     rows, d = out_ref.shape[1], x_ref.shape[1]
-    torus.greet()
+    torus.greet(*torus.far)
 
     def set_input(ref):
         wide = ref[...].astype(F32)
@@ -314,14 +309,16 @@
             dg_acc[...] += dot_nt(dgate, wg)
             du_acc[...] += dot_nt(dup, wu)
         at = at_ref[...]
-        C[c_slot, ..., :chunk] = dot(at, dgate).astype(BF16).reshape(side, side, 2, rows, chunk)
-        C[c_slot, ..., chunk:] = dot(at, dup).astype(BF16).reshape(side, side, 2, rows, chunk)
+        for k, g in enumerate((dgate, dup)):
+            blocks = dot(at, g).astype(BF16).reshape(side, side, 2, rows, chunk)
+            for c in range(2):
+                C[c_slot, c, :, :, :, k * chunk : (k + 1) * chunk] = blocks[:, :, c]
         dwd = lax.dot_general(act, dy, (((0,), (0,)), ((), ())), preferred_element_type=F32).astype(BF16)
         pieces = ff // d
         for b in range(2):
             for k in range(pieces):
                 row = (b * pieces + k) * rows
-                D[1 if inner else 0, lax.div(f, side), lax.rem(f, side), b, :, k * d : (k + 1) * d] = dwd[row : row + rows]
+                D[1 if inner else 0, b, lax.div(f, side), lax.rem(f, side), :, k * d : (k + 1) * d] = dwd[row : row + rows]
 
     def squares(total):
         wide = total.astype(F32)
@@ -329,12 +326,12 @@
 
     def d_view(layer, first, width):
         def view(i, c):
-            return D.at[layer, :, :, c, :, pl.ds(pl.multiple_of((i - first) * width, width), width)]
+            return D.at[layer, c, :, :, :, pl.ds(pl.multiple_of((i - first) * width, width), width)]
 
         return view
 
     def c_view(i, c):
-        return C.at[lax.rem(i, C.shape[0]), :, :, c]
+        return C.at[lax.rem(i, C.shape[0]), c]
 
     def sink_main(i, st, total):
         squares(total)
@@ -400,17 +397,18 @@
 
     lax.fori_loop(0, 2 * steps + tail + 13, body, 0)
 
-    swaps = [torus.partner]
-    for axis in (0, 1):
-        p = torus.at[axis]
-        for q in (p + 1 - 2 * lax.rem(p, 2), side - 1 - p):
-            swaps.append(torus.along(axis, q))
-    for k, other in enumerate(swaps):
-        swap = remote(sqs.at[k], sqr.at[k], qs.at[k], qv.at[k], other)
-        swap.start()
-        swap.wait()
-        sqs[k + 1] = sqs[k] + sqr[k]
-    total = jnp.broadcast_to(jnp.sum(sqs[len(swaps)], keepdims=True), factor_ref.shape)
+    rounds = [[torus.partner]] + [torus.neighbour[axis] + [torus.far[axis]] for axis in (0, 1)]
+    for k, others in enumerate(rounds):
+        swaps = [remote(sqs.at[k], sqr.at[k, j], qs.at[k, j], qv.at[k, j], other) for j, other in enumerate(others)]
+        for swap in swaps:
+            swap.start()
+        for swap in swaps:
+            swap.wait()
+        total = sqs[k]
+        for j in range(len(others)):
+            total = total + sqr[k, j]
+        sqs[k + 1] = total
+    total = jnp.broadcast_to(jnp.sum(sqs[len(rounds)], keepdims=True), factor_ref.shape)
     factor_ref[...] = jnp.minimum(1.0, 0.5 * lax.rsqrt(total / count + 1e-30))
 
 
@@ -435,12 +433,12 @@
             pltpu.VMEM((tokens, d), F32),
             pltpu.VMEM((2, 3, d, chunk), BF16),
             dma((2, 3)),
-            pltpu.VMEM((3, side, side, 2, rows, 2 * chunk), BF16),
-            pltpu.VMEM((2, side, side, 2, rows, ff), BF16),
-            pltpu.VMEM((6, 8, 128), F32),
-            pltpu.VMEM((5, 8, 128), F32),
-            dma((5,)),
-            dma((5,)),
+            pltpu.VMEM((3, 2, side, side, rows, 2 * chunk), BF16),
+            pltpu.VMEM((2, 2, side, side, rows, ff), BF16),
+            pltpu.VMEM((4, 8, 128), F32),
+            pltpu.VMEM((3, 3, 8, 128), F32),
+            dma((3, 3)),
+            dma((3, 3)),
         ]
         + Pipe.scratch(side, rows, 2 * chunk)
         + Pipe.scratch(side, rows, chunk),

time: 459 us -> 454 us (0.989)
  Pallas kernels: 421 us -> 416 us
where the time goes in v4:
time: 454 us
  Pallas kernels  416 us (92%)
  local copies, waits for them, and re-layouts  26.9 us (6%)
  other arithmetic  10.3 us (2%)
    pallas_call x1, Pallas kernels, summed_gradients(): pl.pallas_call(functools.partial(gradient_kernel, side, ff, chunk, sum((t...  245 us
    pallas_call x1, Pallas kernels, gathered(): pl.pallas_call(functools.partial(gather_kernel, side), name='gather_weigh...  139 us
    pallas_call x1, Pallas kernels, forward(): pl.pallas_call(functools.partial(forward_kernel, steps), name='layer_forw...  31.8 us
    unnamed x11, local copies, waits for them, and re-layouts  24.2 us
    convert_element_type x2, other arithmetic, adamw(): return ((w - 0.02 * step).astype(jnp.bfloat16), m, v)  9.58 us

profile of v4, /device:TPU:97, one launch (start us, length us, event | category | flops | bytes accessed | tf_op | source)
XLA Modules:
  0.0 453.9 jit_solution(16671738532685336212)
XLA Ops:
  0.6 31.8 %layer_forward.1.h_ref = bf16[1024,512]{1,0:T(8,128)(2,1)} custom-call(bf16[1024,512]{1,0:T(8,128)(2,1)} %bitcast.26, bf16[2,512,8192]{2,1,0:T(8,128)(2,1)} %wg_hbm.1, bf16[2,512,8192]{2,1,0:T(8,128)(2,1)} %wu_hbm.1, bf16[2,8192,512]{2,1,0:T(8,128)(2,1)} %wd_hbm.1), custom_call_target="tpu_custom_call" | custom-call | flops 25769803776 | bytes 25165824 | tf_op jit(solution)/shard_map/layer_forward/pallas_call | solution.py:54
  32.4 244.8 %summed_gradients.1 = (bf16[6,16,8192]{2,1,0:T(8,128)(2,1)}, f32[8,128]{1,0:T(8,128)}) custom-call(bf16[1024,512]{1,0:T(8,128)(2,1)} %bitcast.27, bf16[1024,512]{1,0:T(8,128)(2,1)} %layer_forward.1.h_ref, bf16[1024,512]{1,0:T(8,128)(2,1)} %bitcast.28, bf16[2,512,8192]{2,1,0:T(8,128)(2,1)} %wg_hbm.1, bf16[2,512,8192]{2,1,0:T(8,128)(2,1)} %wu_hbm.1, ...), custom_call_target="tpu_custom_call" | custom-call | flops 120259084288 | bytes 50331648 | tf_op jit(solution)/shard_map/summed_gradients/pallas_call | solution.py:422
  277.2 1.2 slice.23
  278.4 1.4 fusion.17
  279.9 0.7 convert_multiply_fusion.3
  280.6 0.1 copy.23
  280.7 3.6 fusion.8
  284.2 6.0 %fusion.2 = (bf16[2,16,8192]{2,1,0:T(8,128)(2,1)S(1)}, f32[2,16,8192]{2,1,0:T(8,128)}, f32[2,16,8192]{2,1,0:T(8,128)}, bf16[2,16,8192]{2,1,0:T(8,128)(2,1)S(1)},...) fusion(bf16[2,512,8192]{2,1,0:T(8,128)(2,1)} %wg_hbm.1, s32[]{:T(128)S(6)} %select_n.7, f32[]{:T(128)} %bitcast.2, ...), kind=kLoop, calls=%fused_computation.11 | loop fusion | flops 10485760 | bytes 11534344 | tf_op jit(solution)/shard_map/convert_element_type | solution.py:581
  290.2 139.4 %gather_weights.1 = (bf16[2,4,4,2,16,8192]{5,4,3,2,1,0:T(8,128)(2,1)S(1)}, bf16[2,4,4,2,16,8192]{5,4,3,2,1,0:T(8,128)(2,1)S(1)}, bf16[2,4,4,2,256,512]{5,4,3,2,1,0:T(8,128)(2,1)}) custom-call(bf16[2,16,8192]{2,1,0:T(8,128)(2,1)S(1)} %get-tuple-element.25.own_gate, bf16[2,16,8192]{2,1,0:T(8,128)(2,1)S(1)} %get-tuple-element.34.own_up, ...), custom_call_target="tpu_custom_call" | custom-call | flops 100000000 | bytes 100000000 | tf_op jit(solution)/shard_map/gather_weights/pallas_call | solution.py:564
  429.7 0.0 slice-start
  429.7 0.0 slice-start.1
  429.7 8.5 %copy.27 = bf16[2,512,8192]{2,1,0:T(8,128)(2,1)} copy(bf16[2,512,8192]{2,1,0:T(8,128)(2,1)S(1)} %bitcast.20) | data formatting | bytes 33554432
  438.2 0.0 slice-start.2
  438.2 0.0 slice-start.3
  438.2 8.4 %copy.28 = bf16[2,512,8192]{2,1,0:T(8,128)(2,1)} copy(bf16[2,512,8192]{2,1,0:T(8,128)(2,1)S(1)} %bitcast.19) | data formatting | bytes 33554432
  446.6 0.0 slice-done
  446.6 0.0 slice-done.1
  446.6 0.0 slice-done.2
  446.6 1.1 slice-done.3
  447.7 6.2 %copy.29 = bf16[2,8192,512]{2,1,0:T(8,128)(2,1)} copy(bf16[2,8192,512]{2,1,0:T(8,128)(2,1)S(1)} %bitcast.23) | data formatting | bytes 33554432
  (1 shorter events, 0.0 us)
Async XLA Ops:
  429.7 17.0 %slice-start = ((s8[16777216]{0:T(1024)(128)(4,1)}), s8[4194304]{0:T(1024)(128)(4,1)S(1)}, s32[]{:S(2)}) async-start(s8[16777216]{0:T(1024)(128)(4,1)} %bitcast.21), calls=%async_computation | async-start | bytes 8388608
  429.7 16.9 %slice-start.1 = ((s8[16777216]{0:T(1024)(128)(4,1)}), s8[4194304]{0:T(1024)(128)(4,1)S(1)}, s32[]{:S(2)}) async-start(s8[16777216]{0:T(1024)(128)(4,1)} %bitcast.21), calls=%async_computation.1 | async-start | bytes 8388608
  438.2 8.4 %slice-start.2 = ((s8[16777216]{0:T(1024)(128)(4,1)}), s8[4194304]{0:T(1024)(128)(4,1)S(1)}, s32[]{:S(2)}) async-start(s8[16777216]{0:T(1024)(128)(4,1)} %bitcast.21), calls=%async_computation.2 | async-start | bytes 8388608
  438.2 9.5 %slice-start.3 = ((s8[16777216]{0:T(1024)(128)(4,1)}), s8[4194304]{0:T(1024)(128)(4,1)S(1)}, s32[]{:S(2)}) async-start(s8[16777216]{0:T(1024)(128)(4,1)} %bitcast.21), calls=%async_computation.3 | async-start | bytes 8388608
